TPU v7x, 128 devices: a whole 4x4x4 slice. The times are simulated.
128 devices in a mesh: scene: 8 (over x, core), slab: 16 (over y, z).
Axes of the slice: x: 4, y: 4, z: 4, core: 2. Of those that a mesh axis runs over, the one named last changes fastest.
Arguments:
- camera_features: bfloat16 [8192, 128, 128], P(('scene', 'slab')), parts along dimension 0, may hold values from -6 to 6
- cell_index: int32 [8192, 128], P('scene'), parts along dimension 0, may hold values from 0 to 127
- owner_device: int32 [8192, 1], P('scene'), parts along dimension 0, may hold values from 0 to 15; in each aligned block of 64 rows (0 to 63, 64 to 127, ...) at most 8 rows name the same one
- owner_tile: int32 [8192], P('scene'), parts along dimension 0, may hold values from 0 to 31
- base_map: bfloat16 [2048, 256, 128], P(('scene', 'slab')), parts along dimension 0, may hold values from -6 to 6
- targets: bfloat16 [2048, 256, 128], P(('scene', 'slab')), parts along dimension 0, may hold values from 0 to 1
- fine_conv: bfloat16 [1152, 128], replicated, may hold values from -0.1875 to 0.1875
- fine_down: bfloat16 [512, 256], replicated, may hold values from -0.25 to 0.25
- middle_conv: bfloat16 [2304, 256], replicated, may hold values from -0.125 to 0.125
- middle_down: bfloat16 [1024, 512], replicated, may hold values from -0.1875 to 0.1875
- coarse_conv: bfloat16 [4608, 512], replicated, may hold values from -0.09375 to 0.09375
- coarse_up: bfloat16 [512, 1024], replicated, may hold values from -0.25 to 0.25
- middle_merge: bfloat16 [2304, 256], replicated, may hold values from -0.125 to 0.125
- middle_up: bfloat16 [256, 512], replicated, may hold values from -0.375 to 0.375
- fine_merge: bfloat16 [1152, 128], replicated, may hold values from -0.1875 to 0.1875
- head_weight: bfloat16 [128, 128], replicated, may hold values from -0.5 to 0.5
Outputs:
- camera_grad: bfloat16 [8192, 128, 128], P(('scene', 'slab')), parts along dimension 0
- row_loss: float32 [2048], P(('scene', 'slab')), parts along dimension 0
- fine_conv_grad: float32 [9216, 128], P(('scene', 'slab')), parts along dimension 0
- fine_down_grad: float32 [4096, 256], P(('scene', 'slab')), parts along dimension 0
- middle_conv_grad: float32 [18432, 256], P(('scene', 'slab')), parts along dimension 0
- middle_down_grad: float32 [8192, 512], P(('scene', 'slab')), parts along dimension 0
- coarse_conv_grad: float32 [36864, 512], P(('scene', 'slab')), parts along dimension 0
- coarse_up_grad: float32 [4096, 1024], P(('scene', 'slab')), parts along dimension 0
- middle_merge_grad: float32 [18432, 256], P(('scene', 'slab')), parts along dimension 0
- middle_up_grad: float32 [2048, 512], P(('scene', 'slab')), parts along dimension 0
- fine_merge_grad: float32 [9216, 128], P(('scene', 'slab')), parts along dimension 0
- head_grad: float32 [1024, 128], P(('scene', 'slab')), parts along dimension 0
There are 8 independent parts, one for each index of `scene`. A program takes and returns all parts, laid end to end along the dimension named above; an argument that names none is the same for every part. Nothing has to cross between parts.
Inputs may be any that keep to these rules, and one draw needn't show every extreme that they name: `owner_device`: of the 64 blocks in each aligned run of 64 rows (the blocks of one index of slab), at most 8 name the same index, a bound that some block reaches of them.
All inputs are finite; a program needn't handle non-finite values.
Results may differ from a plain program's by a relative error of at most 0.017.
Values may be sent and summed in bfloat16 or wider, within the bound.
A program may use at most 192 MiB of HBM per device.

v0:
```python
import jax
import jax.numpy as jnp
from jax import lax
from jax.sharding import PartitionSpec as P

BLK_DEV = 64
C1 = 256
C2 = 512
K = 128
TILE = 128
CAP = 8


loss_weight = 0.0625


def extended(block, sides, width):
    for axis, dim in sides:
        count = lax.axis_size(axis)
        forward = [(i, i + 1) for i in range(count - 1)]
        backward = [(target, source) for source, target in forward]
        low = lax.ppermute(
            lax.slice_in_dim(block, block.shape[dim] - width, None, axis=dim), axis, forward
        )
        high = lax.ppermute(lax.slice_in_dim(block, 0, width, axis=dim), axis, backward)
        block = jnp.concatenate([low, block, high], axis=dim)
    return block


def in_blocks(array, dim, size):
    shape = array.shape
    pieces = array.reshape(*shape[:dim], size, shape[dim] // size, *shape[dim + 1 :])
    return jnp.moveaxis(pieces, dim, 0)


def sum_packed(arrays, axis, dims):
    size = lax.axis_size(axis)
    pieces = [in_blocks(a, dim, size) for a, dim in zip(arrays, dims)]
    lines = jnp.concatenate([b.reshape(size, -1) for b in pieces], axis=1)
    extent = max(16, -(-lines.shape[1] // 1024) * 8)
    lines = jnp.pad(lines, ((0, 0), (0, extent * 128 - lines.shape[1]))).reshape(-1, 128)
    ravelled, at, outs = (lax.psum_scatter(lines, axis, tiled=True).reshape(-1), 0, [])
    for b in pieces:
        part = b[0]
        outs.append(ravelled[at : at + part.size].reshape(part.shape))
        at += part.size
    return tuple(outs)


def window_taps(padded):
    height = padded.shape[0] - 2
    across = padded.shape[1]
    framed = jnp.pad(padded, ((0, 0), (1, 1), (0, 0)))
    pieces = [
        framed[1 + row_step : 1 + row_step + height, 1 + column_step : 1 + column_step + across]
        for row_step in (-1, 0, 1)
        for column_step in (-1, 0, 1)
    ]
    return jnp.concatenate(pieces, axis=-1).reshape(height * across, -1)


def flipped(weight):
    inward = weight.shape[0] // 9
    return weight.reshape(9, inward, -1)[::-1].transpose(0, 2, 1).reshape(-1, inward)


def fold_pairs(field):
    height, across, channels = field.shape
    return (
        field.reshape(height // 2, 2, across // 2, 2, channels)
        .transpose(0, 2, 1, 3, 4)
        .reshape(height // 2 * (across // 2), 4 * channels)
    )


def unfold_pairs(matrix, height, across):
    channels = matrix.shape[1] // 4
    return (
        matrix.reshape(height, across, 2, 2, channels)
        .transpose(0, 2, 1, 3, 4)
        .reshape(2 * height, 2 * across, channels)
    )


def silu_slope(signal):
    logistic = jax.nn.sigmoid(signal)
    return logistic * (1.0 + signal * (1.0 - logistic))


def outer(former, latter):
    return lax.dot_general(
        former, latter, (((0,), (0,)), ((), ())), preferred_element_type=jnp.float32
    )


def backward(former, latter):
    return lax.dot_general(
        former, latter, (((1,), (1,)), ((), ())), preferred_element_type=jnp.float32
    )


def rim_conv(field, weight):
    height, across = (field.shape[0], field.shape[1])
    padded = extended(field, (("slab", 0),), 1)
    taps = window_taps(padded)
    result = jnp.dot(taps, weight, preferred_element_type=jnp.float32)
    return (result.reshape(height, across, -1), taps)


def body(
    camera_features,
    cell_index,
    owner_device,
    owner_tile,
    base_map,
    targets,
    fine_conv,
    fine_down,
    middle_conv,
    middle_down,
    coarse_conv,
    coarse_up,
    middle_merge,
    middle_up,
    fine_merge,
    head_weight,
):
    single = jnp.float32
    bfloat = jnp.bfloat16
    device = lax.axis_index("slab")
    devices = lax.axis_size("slab")
    height, across, channels = base_map.shape
    slot_count = devices * CAP
    tile_count = height * across // TILE
    owners = owner_device[:, 0]
    everyone = owners.shape[0]
    choose = (owners[:, None] == jnp.arange(devices, dtype=jnp.int32)[None, :]).astype(jnp.int32)
    grouped = choose.reshape(devices, BLK_DEV, devices)
    earlier = (jnp.cumsum(grouped, axis=1) - grouped).reshape(everyone, devices)
    ranking = jnp.sum(earlier * choose, axis=1)
    sources = jnp.arange(everyone, dtype=jnp.int32) // BLK_DEV
    slot_number = owners * CAP + ranking
    local_slot = lax.dynamic_slice_in_dim(slot_number, device * BLK_DEV, BLK_DEV)
    slot_range = jnp.arange(slot_count, dtype=jnp.int32)
    send_map = (local_slot[None, :] == slot_range[:, None]).astype(bfloat)
    arrival = sources * CAP + ranking
    receive_map = ((arrival[None, :] == slot_range[:, None]) & (owners[None, :] == device)).astype(
        jnp.int32
    )
    tile_onehot = (owner_tile[:, None] == jnp.arange(tile_count, dtype=jnp.int32)[None, :]).astype(
        jnp.int32
    )
    placement = jnp.einsum("bt,sb->ts", tile_onehot, receive_map).astype(bfloat)
    cell_range = jnp.arange(TILE, dtype=jnp.int32)
    local_cells = lax.dynamic_slice_in_dim(cell_index, device * BLK_DEV, BLK_DEV)
    cell_onehot = (local_cells[:, :, None] == cell_range[None, None, :]).astype(bfloat)
    payload = (
        jnp.einsum("bpt,bpc->btc", cell_onehot, camera_features, preferred_element_type=single)
        .astype(bfloat)
        .reshape(BLK_DEV, -1)
    )
    outgoing = (
        jnp.dot(send_map, payload, preferred_element_type=single)
        .astype(bfloat)
        .reshape(devices, CAP, -1)
    )
    incoming = lax.all_to_all(outgoing, "slab", split_axis=0, concat_axis=0, tiled=True).reshape(
        slot_count, -1
    )
    canvas = jnp.dot(placement, incoming, preferred_element_type=single).reshape(
        height, across, channels
    )
    level_zero = (base_map.astype(single) + canvas).astype(bfloat)
    half_height, half_across = (height // 2, across // 2)
    quarter_height, quarter_across = (height // 4, across // 4)
    pre_fine, taps_fine = rim_conv(level_zero, fine_conv)
    hidden_fine = jax.nn.silu(pre_fine).astype(bfloat)
    quarter_fine = fold_pairs(hidden_fine)
    level_one = (
        jnp.dot(quarter_fine, fine_down, preferred_element_type=single)
        .astype(bfloat)
        .reshape(half_height, half_across, C1)
    )
    pre_middle, taps_middle = rim_conv(level_one, middle_conv)
    hidden_middle = jax.nn.silu(pre_middle).astype(bfloat)
    quarter_middle = fold_pairs(hidden_middle)
    level_two = (
        jnp.dot(quarter_middle, middle_down, preferred_element_type=single)
        .astype(bfloat)
        .reshape(quarter_height, quarter_across, C2)
    )
    pre_coarse, taps_coarse = rim_conv(level_two, coarse_conv)
    hidden_coarse = jax.nn.silu(pre_coarse).astype(bfloat)
    lifted = jnp.dot(hidden_coarse.reshape(-1, C2), coarse_up, preferred_element_type=single)
    joined_middle = (
        unfold_pairs(lifted, quarter_height, quarter_across) + hidden_middle.astype(single)
    ).astype(bfloat)
    pre_merge, taps_merge = rim_conv(joined_middle, middle_merge)
    out_middle = jax.nn.silu(pre_merge).astype(bfloat)
    raised = jnp.dot(out_middle.reshape(-1, C1), middle_up, preferred_element_type=single)
    joined_fine = (
        unfold_pairs(raised, half_height, half_across) + hidden_fine.astype(single)
    ).astype(bfloat)
    pre_top, taps_top = rim_conv(joined_fine, fine_merge)
    out_fine = jax.nn.silu(pre_top).astype(bfloat)
    logits = jnp.dot(out_fine.reshape(-1, channels), head_weight, preferred_element_type=single)
    labels = targets.reshape(-1, K).astype(single)
    penalty = jax.nn.softplus(logits) - labels * logits
    row_loss = jnp.sum(penalty.reshape(height, -1), axis=1) / (across * K)
    slope_logits = ((jax.nn.sigmoid(logits) - labels) * loss_weight).astype(bfloat)
    head_grad = outer(out_fine.reshape(-1, channels), slope_logits)
    back_top = (
        backward(slope_logits, head_weight) * silu_slope(pre_top.reshape(-1, channels))
    ).astype(bfloat)
    fine_merge_grad = outer(taps_top, back_top)
    gradient_fine, _ = rim_conv(back_top.reshape(height, across, channels), flipped(fine_merge))
    joined_fine_grad = gradient_fine.astype(bfloat)
    folded_fine_grad = fold_pairs(joined_fine_grad)
    middle_up_grad = outer(out_middle.reshape(-1, C1), folded_fine_grad)
    back_merge = (
        backward(folded_fine_grad, middle_up) * silu_slope(pre_merge.reshape(-1, C1))
    ).astype(bfloat)
    middle_merge_grad = outer(taps_merge, back_merge)
    gradient_middle, _ = rim_conv(
        back_merge.reshape(half_height, half_across, C1), flipped(middle_merge)
    )
    joined_middle_grad = gradient_middle.astype(bfloat)
    folded_middle_grad = fold_pairs(joined_middle_grad)
    coarse_up_grad = outer(hidden_coarse.reshape(-1, C2), folded_middle_grad)
    back_coarse = (
        backward(folded_middle_grad, coarse_up) * silu_slope(pre_coarse.reshape(-1, C2))
    ).astype(bfloat)
    gradient_coarse, _ = rim_conv(
        back_coarse.reshape(quarter_height, quarter_across, C2), flipped(coarse_conv)
    )
    level_two_grad = gradient_coarse.astype(bfloat)
    middle_down_grad = outer(quarter_middle, level_two_grad.reshape(-1, C2))
    spread = unfold_pairs(
        backward(level_two_grad.reshape(-1, C2), middle_down), quarter_height, quarter_across
    )
    back_middle = ((joined_middle_grad.astype(single) + spread) * silu_slope(pre_middle)).astype(
        bfloat
    )
    middle_conv_grad = outer(taps_middle, back_middle.reshape(-1, C1))
    gradient_one, _ = rim_conv(back_middle, flipped(middle_conv))
    level_one_grad = gradient_one.astype(bfloat)
    fine_down_grad = outer(quarter_fine, level_one_grad.reshape(-1, C1))
    spread_fine = unfold_pairs(
        backward(level_one_grad.reshape(-1, C1), fine_down), half_height, half_across
    )
    back_fine = ((joined_fine_grad.astype(single) + spread_fine) * silu_slope(pre_fine)).astype(
        bfloat
    )
    fine_conv_grad = outer(taps_fine, back_fine.reshape(-1, channels))
    gradient_zero, _ = rim_conv(back_fine, flipped(fine_conv))
    level_zero_grad = gradient_zero.astype(bfloat)
    tiles_grad = level_zero_grad.reshape(tile_count, -1)
    slot_grad = jnp.einsum(
        "ts,tl->sl", placement, tiles_grad, preferred_element_type=single
    ).astype(bfloat)
    returned = lax.all_to_all(
        slot_grad.reshape(devices, CAP, -1), "slab", split_axis=0, concat_axis=0, tiled=True
    ).reshape(slot_count, -1)
    own_blocks = jnp.einsum("sb,sl->bl", send_map, returned, preferred_element_type=single).astype(
        bfloat
    )
    camera_grad = jnp.einsum(
        "bpt,btc->bpc",
        cell_onehot,
        own_blocks.reshape(BLK_DEV, TILE, channels),
        preferred_element_type=single,
    ).astype(bfloat)
    coarse_conv_grad = lax.psum_scatter(
        outer(taps_coarse, back_coarse).astype(jnp.bfloat16),
        "slab",
        scatter_dimension=0,
        tiled=True,
    ).astype(jnp.float32)
    reduced = tuple(
        (
            part.astype(jnp.float32)
            for part in sum_packed(
                (
                    fine_conv_grad.astype(jnp.bfloat16),
                    fine_down_grad.astype(jnp.bfloat16),
                    middle_conv_grad.astype(jnp.bfloat16),
                    middle_down_grad.astype(jnp.bfloat16),
                    coarse_up_grad.astype(jnp.bfloat16),
                    middle_merge_grad.astype(jnp.bfloat16),
                    middle_up_grad.astype(jnp.bfloat16),
                    fine_merge_grad.astype(jnp.bfloat16),
                    head_grad.astype(jnp.bfloat16),
                ),
                "slab",
                (0, 0, 0, 0, 0, 0, 0, 0, 0),
            )
        )
    )
    return (
        camera_grad,
        row_loss,
        reduced[0],
        reduced[1],
        reduced[2],
        reduced[3],
        coarse_conv_grad,
        reduced[4],
        reduced[5],
        reduced[6],
        reduced[7],
        reduced[8],
    )


def solution(mesh):
    return jax.shard_map(
        body,
        mesh=mesh,
        in_specs=(
            P(("scene", "slab"), None, None),
            P("scene", None),
            P("scene", None),
            P("scene"),
            P(("scene", "slab"), None, None),
            P(("scene", "slab"), None, None),
            P(),
            P(),
            P(),
            P(),
            P(),
            P(),
            P(),
            P(),
            P(),
            P(),
        ),
        out_specs=(
            P(("scene", "slab"), None, None),
            P(("scene", "slab")),
            P(("scene", "slab"), None),
            P(("scene", "slab"), None),
            P(("scene", "slab"), None),
            P(("scene", "slab"), None),
            P(("scene", "slab"), None),
            P(("scene", "slab"), None),
            P(("scene", "slab"), None),
            P(("scene", "slab"), None),
            P(("scene", "slab"), None),
            P(("scene", "slab"), None),
        ),
        check_vma=False,
    )
```

profile of v0, /device:TPU:46, one launch (start us, length us, event | category | flops | bytes accessed | tf_op | source)
XLA Modules:
  0.0 565.6 jit_solution(3775630644112156128)
XLA Ops:
  15.4 3.6 fusion
  19.0 8.1 %all-to-all-start = ((bf16[16,8,16384]{2,1,0:T(8,128)(2,1)}), bf16[16,8,16384]{2,1,0:T(8,128)(2,1)}, u32[]{:S(2)}, u32[]{:S(2)}) async-start(bf16[16,8,16384]{2,1,0:T(8,128)(2,1)} %fusion), calls=%async_computation | async-start | bytes 8388608 | tf_op jit(solution)/shard_map/all_to_all | solution.py:167
  27.6 52.8 %all-to-all-done = bf16[16,8,16384]{2,1,0:T(8,128)(2,1)} async-done(((bf16[16,8,16384]{2,1,0:T(8,128)(2,1)}), bf16[16,8,16384]{2,1,0:T(8,128)(2,1)}, u32[]{:S(2)}, u32[]{:S(2)}) %all-to-all-start) | async-done | bytes 4194336 | tf_op jit(solution)/shard_map/all_to_all | solution.py:167
  86.6 5.5 collective-permute-start
  94.6 3.8 collective-permute-done.1
  102.0 4.4 multiply_convert_fusion.2
  107.9 6.5 %collective-permute-start.2 = (bf16[1,128,256]{2,1,0:T(8,128)(2,1)S(1)}, bf16[1,128,256]{2,1,0:T(8,128)(2,1)S(1)}, u32[]{:S(2)}, u32[]{:S(2)}) collective-permute-start(bf16[1,128,256]{2,1,0:T(8,128)(2,1)S(1)} %get-tuple-element.36), channel_id=1, source_target_pairs={{0,1},{1,2},{2,3},{3,4},{4,5},{5,6},{6,7},{7,8},{8,9},{9,10},{10,1... | collective-permute-start | bytes 196616 | tf_op jit(solution)/shard_map/ppermute | solution.py:22
  116.4 4.8 reverse_bitcast_fusion
  128.7 4.8 collective-permute-start.4
  138.2 3.5 collective-permute-done.5
  142.3 5.4 multiply_convert_fusion.6
  152.1 4.6 collective-permute-start.6
  160.0 5.0 collective-permute-done.7
  171.5 3.9 collective-permute-start.8
  183.1 6.8 %copy.143 = bf16[9,512,512]{2,1,0:T(8,128)(2,1)} copy(bf16[9,512,512]{1,2,0:T(8,128)(2,1)} %reverse_bitcast_fusion) | data formatting | bytes 9437184 | tf_op jit(solution)/shard_map/transpose | solution.py:64
  202.8 4.6 collective-permute-start.10
  223.6 3.9 convolution_convert_fusion.4
  227.5 4.0 collective-permute-start.12
  245.8 3.9 collective-permute-start.14
  253.4 3.7 collective-permute-done.15
  257.6 3.8 convolution_convert_fusion.15
  267.5 4.8 fusion.8
  272.3 3.9 collective-permute-start.16
  292.0 6.3 %fusion.10 = bf16[1152,128]{1,0:T(8,128)(2,1)S(1)} fusion(bf16[16,256,1152]{2,1,0:T(8,128)(2,1)} %copy-done.42, bf16[16,256,128]{2,1,0:T(8,128)(2,1)S(1)} %multiply_convert_fusion), kind=kOutput, calls=%fused_computation.25 | convolution fusion | flops 1208107008 | bytes 10780672 | tf_op jit(solution)/shard_map/dot_general | solution.py:91
  307.4 5.9 %reshape.363 = bf16[21888,128]{1,0:T(8,128)(2,1)} reshape(bf16[16,175104]{1,0:T(8,128)(2,1)} %constant_dynamic-update-slice_fusion.18) | data formatting | bytes 11206656 | tf_op jit(solution)/shard_map/reshape | solution.py:41
  313.7 5.2 convolution_convert_fusion.3
  318.9 4.1 collective-permute-start.18
  325.2 5.2 collective-permute-done.19
  340.4 12.9 %all-to-all-start.1 = ((bf16[16,8,16384]{2,1,0:T(8,128)(2,1)}), bf16[16,8,16384]{2,1,0:T(8,128)(2,1)}, u32[]{:S(2)}, u32[]{:S(2)}) async-start(bf16[16,8,16384]{2,1,0:T(8,128)(2,1)} %fusion.1), calls=%async_computation.1 | async-start | bytes 8388608 | tf_op jit(solution)/shard_map/all_to_all | solution.py:261
  355.2 44.5 %all-to-all-done.1 = bf16[16,8,16384]{2,1,0:T(8,128)(2,1)} async-done(((bf16[16,8,16384]{2,1,0:T(8,128)(2,1)}), bf16[16,8,16384]{2,1,0:T(8,128)(2,1)}, u32[]{:S(2)}, u32[]{:S(2)}) %all-to-all-start.1) | async-done | bytes 4194336 | tf_op jit(solution)/shard_map/all_to_all | solution.py:261
  406.4 67.9 %all-reduce.13.cloned.1.call-done = bf16[21888,128]{1,0:T(8,128)(2,1)} async-done(((bf16[21888,128]{1,0:T(8,128)(2,1)}), bf16[21888,128]{1,0:T(8,128)(2,1)}) %all-reduce.13.cloned.1.call-update) | async-done | bytes 5603344
  483.6 72.8 %reduce-scatter.2.cloned.1.call-done = bf16[288,512]{1,0:T(8,128)(2,1)} async-done(((bf16[4608,512]{1,0:T(8,128)(2,1)}), bf16[288,512]{1,0:T(8,128)(2,1)}) %reduce-scatter.2.cloned.1.call-update) | async-done | bytes 294928 | tf_op jit(solution)/shard_map/reduce_scatter | solution.py:273
  (357 shorter events, 167.6 us)
Async XLA Ops:
  19.0 8.2 %copy-start.52 = (s32[1024]{0:T(1024)S(1)}, s32[1024]{0:T(1024)}, u32[]{:S(2)}) copy-start(s32[1024]{0:T(1024)} %param.19) | copy-start | bytes 12292
  19.0 61.3 %all-to-all-start = ((bf16[16,8,16384]{2,1,0:T(8,128)(2,1)}), bf16[16,8,16384]{2,1,0:T(8,128)(2,1)}, u32[]{:S(2)}, u32[]{:S(2)}) async-start(bf16[16,8,16384]{2,1,0:T(8,128)(2,1)} %fusion), calls=%async_computation | async-start | bytes 8388608 | tf_op jit(solution)/shard_map/all_to_all | solution.py:167
  27.1 447.2 %all-reduce.13.cloned.1.call-start = ((), (), s32[]{:S(2)}) async-start(), calls=%async_computation.4 | async-start | bytes 11206656
  27.6 52.8 %copy-start.45 = (bf16[32,128]{1,0:T(8,128)(2,1)}, bf16[32,128]{1,0:T(8,128)(2,1)S(1)}, u32[]{:S(2)}) copy-start(bf16[32,128]{1,0:T(8,128)(2,1)S(1)} %convolution_convert_fusion.18) | copy-start | bytes 24580
  86.6 7.9 %collective-permute-start = (bf16[1,256,128]{2,1,0:T(8,128)(2,1)S(1)}, bf16[1,256,128]{2,1,0:T(8,128)(2,1)S(1)}, u32[]{:S(2)}, u32[]{:S(2)}) collective-permute-start(bf16[1,256,128]{2,1,0:T(8,128)(2,1)S(1)} %get-tuple-element.28), channel_id=1, source_target_pairs={{0,1},{1,2},{2,3},{3,4},{4,5},{5,6},{6,7},{7,8},{8,9},{9,10},{10,1... | collective-permute-start | bytes 196616 | tf_op jit(solution)/shard_map/ppermute | solution.py:22
  92.2 6.2 %collective-permute-start.1 = (bf16[1,256,128]{2,1,0:T(8,128)(2,1)S(1)}, bf16[1,256,128]{2,1,0:T(8,128)(2,1)S(1)}, u32[]{:S(2)}, u32[]{:S(2)}) collective-permute-start(bf16[1,256,128]{2,1,0:T(8,128)(2,1)S(1)} %get-tuple-element.29), channel_id=1, source_target_pairs={{1,0},{2,1},{3,2},{4,3},{5,4},{6,5},{7,6},{8,7},{9,8},{10,9},{11,1... | collective-permute-start | bytes 196616 | tf_op jit(solution)/shard_map/ppermute | solution.py:25
  107.4 13.8 %copy-start.24 = (bf16[8,2,128,2,128]{2,0,4,3,1:T(8,128)(2,1)}, bf16[8,2,128,2,128]{2,0,4,3,1:T(8,128)(2,1)S(1)}, u32[]{:S(2)}) copy-start(bf16[8,2,128,2,128]{2,0,4,3,1:T(8,128)(2,1)S(1)} %copy.132) | copy-start | bytes 3145732
  107.9 13.2 %collective-permute-start.2 = (bf16[1,128,256]{2,1,0:T(8,128)(2,1)S(1)}, bf16[1,128,256]{2,1,0:T(8,128)(2,1)S(1)}, u32[]{:S(2)}, u32[]{:S(2)}) collective-permute-start(bf16[1,128,256]{2,1,0:T(8,128)(2,1)S(1)} %get-tuple-element.36), channel_id=1, source_target_pairs={{0,1},{1,2},{2,3},{3,4},{4,5},{5,6},{6,7},{7,8},{8,9},{9,10},{10,1... | collective-permute-start | bytes 196616 | tf_op jit(solution)/shard_map/ppermute | solution.py:22
  114.5 8.3 %collective-permute-start.3 = (bf16[1,128,256]{2,1,0:T(8,128)(2,1)S(1)}, bf16[1,128,256]{2,1,0:T(8,128)(2,1)S(1)}, u32[]{:S(2)}, u32[]{:S(2)}) collective-permute-start(bf16[1,128,256]{2,1,0:T(8,128)(2,1)S(1)} %get-tuple-element.37), channel_id=1, source_target_pairs={{1,0},{2,1},{3,2},{4,3},{5,4},{6,5},{7,6},{8,7},{9,8},{10,9},{11,1... | collective-permute-start | bytes 196616 | tf_op jit(solution)/shard_map/ppermute | solution.py:25
  128.7 9.5 %collective-permute-start.4 = (bf16[1,64,512]{2,1,0:T(8,128)(2,1)S(1)}, bf16[1,64,512]{2,1,0:T(8,128)(2,1)S(1)}, u32[]{:S(2)}, u32[]{:S(2)}) collective-permute-start(bf16[1,64,512]{2,1,0:T(8,128)(2,1)S(1)} %get-tuple-element.48), channel_id=1, source_target_pairs={{0,1},{1,2},{2,3},{3,4},{4,5},{5,6},{6,7},{7,8},{8,9},{9,10},{10,1... | collective-permute-start | bytes 196616 | tf_op jit(solution)/shard_map/ppermute | solution.py:22
  133.5 8.3 %collective-permute-start.5 = (bf16[1,64,512]{2,1,0:T(8,128)(2,1)S(1)}, bf16[1,64,512]{2,1,0:T(8,128)(2,1)S(1)}, u32[]{:S(2)}, u32[]{:S(2)}) collective-permute-start(bf16[1,64,512]{2,1,0:T(8,128)(2,1)S(1)} %get-tuple-element.49), channel_id=1, source_target_pairs={{1,0},{2,1},{3,2},{4,3},{5,4},{6,5},{7,6},{8,7},{9,8},{10,9},{11,1... | collective-permute-start | bytes 196616 | tf_op jit(solution)/shard_map/ppermute | solution.py:25
  152.1 7.9 %collective-permute-start.6 = (bf16[1,128,256]{2,1,0:T(8,128)(2,1)S(1)}, bf16[1,128,256]{2,1,0:T(8,128)(2,1)S(1)}, u32[]{:S(2)}, u32[]{:S(2)}) collective-permute-start(bf16[1,128,256]{2,1,0:T(8,128)(2,1)S(1)} %get-tuple-element.34), channel_id=1, source_target_pairs={{0,1},{1,2},{2,3},{3,4},{4,5},{5,6},{6,7},{7,8},{8,9},{9,10},{10,1... | collective-permute-start | bytes 196616 | tf_op jit(solution)/shard_map/ppermute | solution.py:22
  156.7 8.3 %collective-permute-start.7 = (bf16[1,128,256]{2,1,0:T(8,128)(2,1)S(1)}, bf16[1,128,256]{2,1,0:T(8,128)(2,1)S(1)}, u32[]{:S(2)}, u32[]{:S(2)}) collective-permute-start(bf16[1,128,256]{2,1,0:T(8,128)(2,1)S(1)} %get-tuple-element.35), channel_id=1, source_target_pairs={{1,0},{2,1},{3,2},{4,3},{5,4},{6,5},{7,6},{8,7},{9,8},{10,9},{11,1... | collective-permute-start | bytes 196616 | tf_op jit(solution)/shard_map/ppermute | solution.py:25
  171.5 18.4 %collective-permute-start.8 = (bf16[1,256,128]{2,1,0:T(8,128)(2,1)S(1)}, bf16[1,256,128]{2,1,0:T(8,128)(2,1)S(1)}, u32[]{:S(2)}, u32[]{:S(2)}) collective-permute-start(bf16[1,256,128]{2,1,0:T(8,128)(2,1)S(1)} %get-tuple-element.26), channel_id=1, source_target_pairs={{0,1},{1,2},{2,3},{3,4},{4,5},{5,6},{6,7},{7,8},{8,9},{9,10},{10,1... | collective-permute-start | bytes 196616 | tf_op jit(solution)/shard_map/ppermute | solution.py:22
  175.4 14.5 %collective-permute-start.9 = (bf16[1,256,128]{2,1,0:T(8,128)(2,1)S(1)}, bf16[1,256,128]{2,1,0:T(8,128)(2,1)S(1)}, u32[]{:S(2)}, u32[]{:S(2)}) collective-permute-start(bf16[1,256,128]{2,1,0:T(8,128)(2,1)S(1)} %get-tuple-element.27), channel_id=1, source_target_pairs={{1,0},{2,1},{3,2},{4,3},{5,4},{6,5},{7,6},{8,7},{9,8},{10,9},{11,1... | collective-permute-start | bytes 196616 | tf_op jit(solution)/shard_map/ppermute | solution.py:25
  202.8 9.9 %collective-permute-start.10 = (bf16[1,256,128]{2,1,0:T(8,128)(2,1)S(1)}, bf16[1,256,128]{2,1,0:T(8,128)(2,1)S(1)}, u32[]{:S(2)}, u32[]{:S(2)}) collective-permute-start(bf16[1,256,128]{2,1,0:T(8,128)(2,1)S(1)} %get-tuple-element.24), channel_id=1, source_target_pairs={{0,1},{1,2},{2,3},{3,4},{4,5},{5,6},{6,7},{7,8},{8,9},{9,10},{10,1... | collective-permute-start | bytes 196616 | tf_op jit(solution)/shard_map/ppermute | solution.py:22
  207.4 6.2 %collective-permute-start.11 = (bf16[1,256,128]{2,1,0:T(8,128)(2,1)S(1)}, bf16[1,256,128]{2,1,0:T(8,128)(2,1)S(1)}, u32[]{:S(2)}, u32[]{:S(2)}) collective-permute-start(bf16[1,256,128]{2,1,0:T(8,128)(2,1)S(1)} %get-tuple-element.25), channel_id=1, source_target_pairs={{1,0},{2,1},{3,2},{4,3},{5,4},{6,5},{7,6},{8,7},{9,8},{10,9},{11,1... | collective-permute-start | bytes 196616 | tf_op jit(solution)/shard_map/ppermute | solution.py:25
  223.6 10.0 %copy-start.27 = (bf16[8,2,128,2,128]{2,0,4,3,1:T(8,128)(2,1)S(1)}, bf16[8,2,128,2,128]{2,0,4,3,1:T(8,128)(2,1)}, u32[]{:S(2)}) copy-start(bf16[8,2,128,2,128]{2,0,4,3,1:T(8,128)(2,1)} %copy-done.26) | copy-start | bytes 3145732
  227.5 8.9 %collective-permute-start.12 = (bf16[1,128,256]{2,1,0:T(8,128)(2,1)S(1)}, bf16[1,128,256]{2,1,0:T(8,128)(2,1)S(1)}, u32[]{:S(2)}, u32[]{:S(2)}) collective-permute-start(bf16[1,128,256]{2,1,0:T(8,128)(2,1)S(1)} %get-tuple-element.32), channel_id=1, source_target_pairs={{0,1},{1,2},{2,3},{3,4},{4,5},{5,6},{6,7},{7,8},{8,9},{9,10},{10,1... | collective-permute-start | bytes 196616 | tf_op jit(solution)/shard_map/ppermute | solution.py:22
  231.6 8.3 %collective-permute-start.13 = (bf16[1,128,256]{2,1,0:T(8,128)(2,1)S(1)}, bf16[1,128,256]{2,1,0:T(8,128)(2,1)S(1)}, u32[]{:S(2)}, u32[]{:S(2)}) collective-permute-start(bf16[1,128,256]{2,1,0:T(8,128)(2,1)S(1)} %get-tuple-element.33), channel_id=1, source_target_pairs={{1,0},{2,1},{3,2},{4,3},{5,4},{6,5},{7,6},{8,7},{9,8},{10,9},{11,1... | collective-permute-start | bytes 196616 | tf_op jit(solution)/shard_map/ppermute | solution.py:25
  245.8 7.7 %collective-permute-start.14 = (bf16[1,64,512]{2,1,0:T(8,128)(2,1)S(1)}, bf16[1,64,512]{2,1,0:T(8,128)(2,1)S(1)}, u32[]{:S(2)}, u32[]{:S(2)}) collective-permute-start(bf16[1,64,512]{2,1,0:T(8,128)(2,1)S(1)} %get-tuple-element.44), channel_id=1, source_target_pairs={{0,1},{1,2},{2,3},{3,4},{4,5},{5,6},{6,7},{7,8},{8,9},{9,10},{10,1... | collective-permute-start | bytes 196616 | tf_op jit(solution)/shard_map/ppermute | solution.py:22
  249.7 7.4 %collective-permute-start.15 = (bf16[1,64,512]{2,1,0:T(8,128)(2,1)S(1)}, bf16[1,64,512]{2,1,0:T(8,128)(2,1)S(1)}, u32[]{:S(2)}, u32[]{:S(2)}) collective-permute-start(bf16[1,64,512]{2,1,0:T(8,128)(2,1)S(1)} %get-tuple-element.45), channel_id=1, source_target_pairs={{1,0},{2,1},{3,2},{4,3},{5,4},{6,5},{7,6},{8,7},{9,8},{10,9},{11,1... | collective-permute-start | bytes 196616 | tf_op jit(solution)/shard_map/ppermute | solution.py:25
  267.5 10.9 %copy-start.23 = (bf16[4,64,512]{2,1,0:T(8,128)(2,1)S(1)}, bf16[4,64,512]{2,1,0:T(8,128)(2,1)}, u32[]{:S(2)}) copy-start(bf16[4,64,512]{2,1,0:T(8,128)(2,1)} %copy-done.22) | copy-start | bytes 786436
  272.3 9.5 %collective-permute-start.16 = (bf16[1,128,256]{2,1,0:T(8,128)(2,1)S(1)}, bf16[1,128,256]{2,1,0:T(8,128)(2,1)S(1)}, u32[]{:S(2)}, u32[]{:S(2)}) collective-permute-start(bf16[1,128,256]{2,1,0:T(8,128)(2,1)S(1)} %get-tuple-element.30), channel_id=1, source_target_pairs={{0,1},{1,2},{2,3},{3,4},{4,5},{5,6},{6,7},{7,8},{8,9},{9,10},{10,1... | collective-permute-start | bytes 196616 | tf_op jit(solution)/shard_map/ppermute | solution.py:22
  276.3 6.9 %collective-permute-start.17 = (bf16[1,128,256]{2,1,0:T(8,128)(2,1)S(1)}, bf16[1,128,256]{2,1,0:T(8,128)(2,1)S(1)}, u32[]{:S(2)}, u32[]{:S(2)}) collective-permute-start(bf16[1,128,256]{2,1,0:T(8,128)(2,1)S(1)} %get-tuple-element.31), channel_id=1, source_target_pairs={{1,0},{2,1},{3,2},{4,3},{5,4},{6,5},{7,6},{8,7},{9,8},{10,9},{11,1... | collective-permute-start | bytes 196616 | tf_op jit(solution)/shard_map/ppermute | solution.py:25
  313.4 243.1 %reduce-scatter.2.cloned.1.call-start = ((), (), s32[]{:S(2)}) async-start(), calls=%async_computation.3 | async-start | bytes 5013504 | tf_op jit(solution)/shard_map/reduce_scatter | solution.py:273
  318.9 6.3 %collective-permute-start.18 = (bf16[1,256,128]{2,1,0:T(8,128)(2,1)S(1)}, bf16[1,256,128]{2,1,0:T(8,128)(2,1)S(1)}, u32[]{:S(2)}, u32[]{:S(2)}) collective-permute-start(bf16[1,256,128]{2,1,0:T(8,128)(2,1)S(1)} %get-tuple-element.22), channel_id=1, source_target_pairs={{0,1},{1,2},{2,3},{3,4},{4,5},{5,6},{6,7},{7,8},{8,9},{9,10},{10,1... | collective-permute-start | bytes 196616 | tf_op jit(solution)/shard_map/ppermute | solution.py:22
  323.0 7.5 %collective-permute-start.19 = (bf16[1,256,128]{2,1,0:T(8,128)(2,1)S(1)}, bf16[1,256,128]{2,1,0:T(8,128)(2,1)S(1)}, u32[]{:S(2)}, u32[]{:S(2)}) collective-permute-start(bf16[1,256,128]{2,1,0:T(8,128)(2,1)S(1)} %get-tuple-element.23), channel_id=1, source_target_pairs={{1,0},{2,1},{3,2},{4,3},{5,4},{6,5},{7,6},{8,7},{9,8},{10,9},{11,1... | collective-permute-start | bytes 196616 | tf_op jit(solution)/shard_map/ppermute | solution.py:25
  340.4 12.9 %copy-start.53 = (u32[128]{0:T(128)S(1)}, u32[128]{0:T(128)}, u32[]{:S(2)}) copy-start(u32[128]{0:T(128)} %constant.82) | copy-start | bytes 1540
  340.4 59.3 %copy-start.49 = (s32[64]{0:T(128)S(1)}, s32[64]{0:T(128)}, u32[]{:S(2)}) copy-start(s32[64]{0:T(128)} %copy-done.48) | copy-start | bytes 772
  340.4 59.3 %all-to-all-start.1 = ((bf16[16,8,16384]{2,1,0:T(8,128)(2,1)}), bf16[16,8,16384]{2,1,0:T(8,128)(2,1)}, u32[]{:S(2)}, u32[]{:S(2)}) async-start(bf16[16,8,16384]{2,1,0:T(8,128)(2,1)} %fusion.1), calls=%async_computation.1 | async-start | bytes 8388608 | tf_op jit(solution)/shard_map/all_to_all | solution.py:261
  403.4 154.9 %copy-start.1 = (bf16[64,128,128]{2,1,0:T(8,128)(2,1)S(1)}, bf16[64,128,128]{2,1,0:T(8,128)(2,1)}, u32[]{:S(2)}) copy-start(bf16[64,128,128]{2,1,0:T(8,128)(2,1)} %param.16) | copy-start | bytes 6291460
  (47 other events, 145.0 us)
Sparse Core Ops, SparseCore 0:
  313.5 160.7 all-reduce.12
  477.6 78.7 reduce-scatter.1
where the time goes:
time: 574 us; the launch traced here: 566 us
  waiting for transfers between devices  266 us (46%)
  local copies, waits for them, and re-layouts  89.1 us (16%)
  starting transfers between devices  87.8 us (15%)
  matrix products  85 us (15%)
  other arithmetic  20.3 us (4%)
  between operations  17 us (3%)
    reduce_scatter x1, waiting for transfers between devices, body(): lax.psum_scatter(outer(taps_coarse, back_coarse).astype(jnp.bfloat16), 's...  72.8 us
    unnamed x3, waiting for transfers between devices  68 us
    all_to_all x1, waiting for transfers between devices, body(): lax.all_to_all(outgoing, 'slab', split_axis=0, concat_axis=0, tiled=True)  52.8 us
    ppermute x10, starting transfers between devices, extended(): lax.ppermute(lax.slice_in_dim(block, block.shape[dim] - width, None, axis...  45.9 us
    all_to_all x1, waiting for transfers between devices, body(): lax.all_to_all(slot_grad.reshape(devices, CAP, -1), 'slab', split_axis=0,...  44.5 us
    dot_general x10, matrix products, rim_conv(): result = jnp.dot(taps, weight, preferred_element_type=jnp.float32)  29.4 us
    ppermute x10, waiting for transfers between devices, extended(): lax.ppermute(lax.slice_in_dim(block, 0, width, axis=dim), axis, backward)  28.4 us
    unnamed x183, local copies, waits for them, and re-layouts  27.1 us
  transfers between devices with their start and end apart: 24, of which 13 were waited for; matrix products, arithmetic and copies ran while one was open for 11% of the time, Pallas kernels for 0%

commit v1 on v0

--- a/solution.py
+++ b/solution.py
@@ -2,6 +2,7 @@
 import jax.numpy as jnp
 from jax import lax
 from jax.sharding import PartitionSpec as P
+
 
 BLK_DEV = 64
 C1 = 256
@@ -27,24 +28,40 @@
     return block
 
 
-def in_blocks(array, dim, size):
-    shape = array.shape
-    pieces = array.reshape(*shape[:dim], size, shape[dim] // size, *shape[dim + 1 :])
-    return jnp.moveaxis(pieces, dim, 0)
-
-
-def sum_packed(arrays, axis, dims):
+def as_lines(block, width):
+    rows, columns = block.shape[-2], block.shape[-1]
+    if columns >= width:
+        parts = [block[..., at : at + width] for at in range(0, columns, width)]
+        return jnp.concatenate(parts, axis=-2)
+    step = rows * columns // width
+    parts = [block[..., at : at + step, :] for at in range(0, rows, step)]
+    return jnp.concatenate(parts, axis=-1)
+
+
+def from_lines(lines, rows, columns):
+    width = lines.shape[1]
+    if columns >= width:
+        return jnp.concatenate([lines[at : at + rows] for at in range(0, lines.shape[0], rows)], 1)
+    return jnp.concatenate([lines[:, at : at + columns] for at in range(0, width, columns)], 0)
+
+
+def sum_packed(arrays, axis, width=512):
     size = lax.axis_size(axis)
-    pieces = [in_blocks(a, dim, size) for a, dim in zip(arrays, dims)]
-    lines = jnp.concatenate([b.reshape(size, -1) for b in pieces], axis=1)
-    extent = max(16, -(-lines.shape[1] // 1024) * 8)
-    lines = jnp.pad(lines, ((0, 0), (0, extent * 128 - lines.shape[1]))).reshape(-1, 128)
-    ravelled, at, outs = (lax.psum_scatter(lines, axis, tiled=True).reshape(-1), 0, [])
-    for b in pieces:
-        part = b[0]
-        outs.append(ravelled[at : at + part.size].reshape(part.shape))
-        at += part.size
-    return tuple(outs)
+    shapes = [(array.shape[0] // size, array.shape[1]) for array in arrays]
+    pieces = [as_lines(a.reshape(size, *shape), width) for a, shape in zip(arrays, shapes)]
+    total = sum(piece.shape[1] for piece in pieces)
+    spare = -total % 16
+    if spare:
+        pieces.append(jnp.zeros((size, spare, width), arrays[0].dtype))
+    lines = lax.optimization_barrier(jnp.concatenate(pieces, axis=1).reshape(-1, width))
+    summed = lax.psum_scatter(lines, axis, scatter_dimension=0, tiled=True)
+    summed = lax.optimization_barrier(summed)
+    at, outs = 0, []
+    for rows, columns in shapes:
+        count = rows * columns // width
+        outs.append(from_lines(summed[at : at + count], rows, columns).astype(jnp.float32))
+        at += count
+    return outs
 
 
 def window_taps(padded):
@@ -230,6 +247,28 @@
     back_coarse = (
         backward(folded_middle_grad, coarse_up) * silu_slope(pre_coarse.reshape(-1, C2))
     ).astype(bfloat)
+    coarse_conv_grad = outer(taps_coarse, back_coarse)
+    (
+        coarse_conv_sum,
+        coarse_up_sum,
+        middle_merge_sum,
+        middle_up_sum,
+        fine_merge_sum,
+        head_sum,
+    ) = sum_packed(
+        [
+            g.astype(bfloat)
+            for g in (
+                coarse_conv_grad,
+                coarse_up_grad,
+                middle_merge_grad,
+                middle_up_grad,
+                fine_merge_grad,
+                head_grad,
+            )
+        ],
+        "slab",
+    )
     gradient_coarse, _ = rim_conv(
         back_coarse.reshape(quarter_height, quarter_across, C2), flipped(coarse_conv)
     )
@@ -252,6 +291,13 @@
         bfloat
     )
     fine_conv_grad = outer(taps_fine, back_fine.reshape(-1, channels))
+    middle_down_sum, middle_conv_sum, fine_down_sum, fine_conv_sum = sum_packed(
+        [
+            g.astype(bfloat)
+            for g in (middle_down_grad, middle_conv_grad, fine_down_grad, fine_conv_grad)
+        ],
+        "slab",
+    )
     gradient_zero, _ = rim_conv(back_fine, flipped(fine_conv))
     level_zero_grad = gradient_zero.astype(bfloat)
     tiles_grad = level_zero_grad.reshape(tile_count, -1)
@@ -270,45 +316,19 @@
         own_blocks.reshape(BLK_DEV, TILE, channels),
         preferred_element_type=single,
     ).astype(bfloat)
-    coarse_conv_grad = lax.psum_scatter(
-        outer(taps_coarse, back_coarse).astype(jnp.bfloat16),
-        "slab",
-        scatter_dimension=0,
-        tiled=True,
-    ).astype(jnp.float32)
-    reduced = tuple(
-        (
-            part.astype(jnp.float32)
-            for part in sum_packed(
-                (
-                    fine_conv_grad.astype(jnp.bfloat16),
-                    fine_down_grad.astype(jnp.bfloat16),
-                    middle_conv_grad.astype(jnp.bfloat16),
-                    middle_down_grad.astype(jnp.bfloat16),
-                    coarse_up_grad.astype(jnp.bfloat16),
-                    middle_merge_grad.astype(jnp.bfloat16),
-                    middle_up_grad.astype(jnp.bfloat16),
-                    fine_merge_grad.astype(jnp.bfloat16),
-                    head_grad.astype(jnp.bfloat16),
-                ),
-                "slab",
-                (0, 0, 0, 0, 0, 0, 0, 0, 0),
-            )
-        )
-    )
     return (
         camera_grad,
         row_loss,
-        reduced[0],
-        reduced[1],
-        reduced[2],
-        reduced[3],
-        coarse_conv_grad,
-        reduced[4],
-        reduced[5],
-        reduced[6],
-        reduced[7],
-        reduced[8],
+        fine_conv_sum,
+        fine_down_sum,
+        middle_conv_sum,
+        middle_down_sum,
+        coarse_conv_sum,
+        coarse_up_sum,
+        middle_merge_sum,
+        middle_up_sum,
+        fine_merge_sum,
+        head_sum,
     )
 
 

time: 574 us -> 517 us (0.901)
  waiting for transfers between devices: 266 us -> 183 us
  local copies, waits for them, and re-layouts: 89.1 us -> 116 us
  other arithmetic: 20.3 us -> 26.8 us
  matrix products: 85 us -> 78.7 us
    unnamed x3 -> x2, waiting for transfers between devices: 68 us -> 0.03 us
    concatenate x1 -> x2, local copies, waits for them, and re-layouts: 0.62 us -> 47.6 us  [sum_packed(): jnp.concatenate(pieces, axis=1).reshape(-1, width)]
    reduce_scatter x1 -> x2, waiting for transfers between devices: 72.8 us -> 49.7 us  [sum_packed(): summed = lax.psum_scatter(lines, axis, scatter_dimension=0, tiled=True)]
    another operation x9 -> x0, local copies, waits for them, and re-layouts: 9.91 us -> none  [sum_packed(): lines = jnp.concatenate([b.reshape(size, -1) for b in pieces], axis=1)]
    reshape x1 -> x0, local copies, waits for them, and re-layouts: 5.93 us -> none  [sum_packed(): jnp.pad(lines, ((0, 0), (0, extent * 128 - lines.shape[1])))]
    slice x0 -> x14, local copies, waits for them, and re-layouts: none -> 5.81 us  [the longest x6 4.5 us: from_lines(): lines[:, at:at + columns]]
    unnamed x183 -> x192, local copies, waits for them, and re-layouts: 27.1 us -> 24.3 us
  transfers between devices with their start and end apart: 24 -> 24, of which waited for: 13 -> 13; matrix products, arithmetic and copies ran while one was open for 11% -> 19% of each run, Pallas kernels for 0% -> 0%
where the time goes in v1:
time: 517 us; the launch traced here: 507 us
  waiting for transfers between devices  183 us (35%)
  local copies, waits for them, and re-layouts  116 us (22%)
  starting transfers between devices  86 us (17%)
  matrix products  78.7 us (15%)
  other arithmetic  26.8 us (5%)
  between operations  16.3 us (3%)
    all_to_all x1, waiting for transfers between devices, body(): lax.all_to_all(outgoing, 'slab', split_axis=0, concat_axis=0, tiled=True)  52.8 us
    reduce_scatter x2, waiting for transfers between devices, sum_packed(): summed = lax.psum_scatter(lines, axis, scatter_dimension=0, tiled=True)  49.7 us
    concatenate x2, local copies, waits for them, and re-layouts, sum_packed(): jnp.concatenate(pieces, axis=1).reshape(-1, width)  47.6 us
    all_to_all x1, waiting for transfers between devices, body(): lax.all_to_all(slot_grad.reshape(devices, CAP, -1), 'slab', split_axis=0,...  46.5 us
    ppermute x10, starting transfers between devices, extended(): lax.ppermute(lax.slice_in_dim(block, block.shape[dim] - width, None, axis...  46.1 us
    ppermute x10, waiting for transfers between devices, extended(): lax.ppermute(lax.slice_in_dim(block, 0, width, axis=dim), axis, backward)  33.8 us
    dot_general x10, matrix products, outer(): lax.dot_general(former, latter, (((0,), (0,)), ((), ())), preferred_eleme...  25.7 us
    unnamed x192, local copies, waits for them, and re-layouts  24.3 us
  transfers between devices with their start and end apart: 24, of which 13 were waited for; matrix products, arithmetic and copies ran while one was open for 19% of the time, Pallas kernels for 0%

profile of v1, /device:TPU:46, one launch (start us, length us, event | category | flops | bytes accessed | tf_op | source)
XLA Modules:
  0.0 506.9 jit_solution(6702370576961119098)
XLA Ops:
  12.4 3.0 fusion.19
  15.4 3.6 fusion
  19.0 8.1 %all-to-all-start = ((bf16[16,8,16384]{2,1,0:T(8,128)(2,1)}), bf16[16,8,16384]{2,1,0:T(8,128)(2,1)}, u32[]{:S(2)}, u32[]{:S(2)}) async-start(bf16[16,8,16384]{2,1,0:T(8,128)(2,1)} %fusion), calls=%async_computation | async-start | bytes 8388608 | tf_op jit(solution)/shard_map/all_to_all | solution.py:184
  27.6 52.8 %all-to-all-done = bf16[16,8,16384]{2,1,0:T(8,128)(2,1)} async-done(((bf16[16,8,16384]{2,1,0:T(8,128)(2,1)}), bf16[16,8,16384]{2,1,0:T(8,128)(2,1)}, u32[]{:S(2)}, u32[]{:S(2)}) %all-to-all-start) | async-done | bytes 4194336 | tf_op jit(solution)/shard_map/all_to_all | solution.py:184
  86.6 5.5 %collective-permute-start = (bf16[1,256,128]{2,1,0:T(8,128)(2,1)S(1)}, bf16[1,256,128]{2,1,0:T(8,128)(2,1)S(1)}, u32[]{:S(2)}, u32[]{:S(2)}) collective-permute-start(bf16[1,256,128]{2,1,0:T(8,128)(2,1)S(1)} %get-tuple-element.26), channel_id=1, source_target_pairs={{0,1},{1,2},{2,3},{3,4},{4,5},{5,6},{6,7},{7,8},{8,9},{9,10},{10,1... | collective-permute-start | bytes 196616 | tf_op jit(solution)/shard_map/ppermute | solution.py:23
  94.4 3.9 collective-permute-done.1
  102.0 4.4 multiply_convert_fusion.2
  107.9 6.5 %collective-permute-start.2 = (bf16[1,128,256]{2,1,0:T(8,128)(2,1)S(1)}, bf16[1,128,256]{2,1,0:T(8,128)(2,1)S(1)}, u32[]{:S(2)}, u32[]{:S(2)}) collective-permute-start(bf16[1,128,256]{2,1,0:T(8,128)(2,1)S(1)} %get-tuple-element.34), channel_id=1, source_target_pairs={{0,1},{1,2},{2,3},{3,4},{4,5},{5,6},{6,7},{7,8},{8,9},{9,10},{10,1... | collective-permute-start | bytes 196616 | tf_op jit(solution)/shard_map/ppermute | solution.py:23
  116.4 6.3 %collective-permute-done.3 = bf16[1,128,256]{2,1,0:T(8,128)(2,1)S(1)} collective-permute-done((bf16[1,128,256]{2,1,0:T(8,128)(2,1)S(1)}, bf16[1,128,256]{2,1,0:T(8,128)(2,1)S(1)}, u32[]{:S(2)}, u32[]{:S(2)}) %collective-permute-start.3) | collective-permute-done | bytes 65568 | tf_op jit(solution)/shard_map/ppermute | solution.py:26
  129.2 4.8 collective-permute-start.4
  138.0 4.2 collective-permute-done.5
  151.1 3.9 collective-permute-start.6
  157.3 5.9 %collective-permute-done.7 = bf16[1,128,256]{2,1,0:T(8,128)(2,1)S(1)} collective-permute-done((bf16[1,128,256]{2,1,0:T(8,128)(2,1)S(1)}, bf16[1,128,256]{2,1,0:T(8,128)(2,1)S(1)}, u32[]{:S(2)}, u32[]{:S(2)}) %collective-permute-start.7) | collective-permute-done | bytes 65568 | tf_op jit(solution)/shard_map/ppermute | solution.py:26
  169.7 3.9 collective-permute-start.8
  190.0 3.9 collective-permute-start.10
  196.4 3.9 collective-permute-done.11
  210.3 3.9 collective-permute-start.12
  227.9 3.9 collective-permute-start.14
  235.3 6.6 %copy.143 = bf16[9,512,512]{2,1,0:T(8,128)(2,1)} copy(bf16[9,512,512]{1,2,0:T(8,128)(2,1)} %reverse_bitcast_fusion) | data formatting | bytes 9437184 | tf_op jit(solution)/shard_map/transpose | solution.py:81
  254.4 3.8 fusion.8
  258.2 4.2 collective-permute-start.16
  279.0 14.8 %concatenate.233 = bf16[16,176,512]{2,1,0:T(8,128)(2,1)} concatenate(bf16[16,64,512]{2,1,0:T(8,128)(2,1)} %bitcast.286, bf16[16,72,512]{2,1,0:T(8,128)(2,1)} %pad_maximum_fusion, bf16[16,16,512]{2,1,0:T(8,128)(2,1)S(1)} %pad_maximum_fusion.24, bf16[16,18,512]{2,1,0:T(8,128)(2,1)S(1)} %pad_maximum_fusion.18, bf16[16,6,512]{2,1,0:T(8,128)(2,1)} %broadcast_in_dim.4), dimensions={1} | concatenate | bytes 5767168 | tf_op jit(solution)/shard_map/concatenate | solution.py:56
  296.2 6.3 %convolution_convert_fusion.5 = bf16[1152,128]{1,0:T(8,128)(2,1)S(1)} fusion(bf16[4096,1152]{1,0:T(8,128)(2,1)} %bitcast.328, bf16[4096,128]{1,0:T(8,128)(2,1)S(1)} %fusion.2), kind=kOutput, calls=%fused_computation.26 | convolution fusion | flops 1208107008 | bytes 10780672 | tf_op jit(solution)/shard_map/dot_general | solution.py:108
  303.4 3.8 convolution_convert_fusion.4
  311.9 3.7 convolution_convert_fusion.3
  315.6 32.8 %concatenate.240 = bf16[16,464,512]{2,1,0:T(8,128)(2,1)} concatenate(bf16[16,288,512]{2,1,0:T(8,128)(2,1)} %bitcast.253, bf16[16,32,512]{2,1,0:T(8,128)(2,1)S(1)} %get-tuple-element.19, bf16[16,32,512]{2,1,0:T(8,128)(2,1)S(1)} %get-tuple-element.18, bf16[16,72,512]{2,1,0:T(8,128)(2,1)} %pad_maximum_fusion.1, bf16[16,16,512]{2,1,0:T(8,128)(2,1)S(1)} %bitcast.324, ...), dimensions={1} | concatenate | bytes 15204352 | tf_op jit(solution)/shard_map/concatenate | solution.py:56
  348.4 5.5 %collective-permute-start.18 = (bf16[1,256,128]{2,1,0:T(8,128)(2,1)S(1)}, bf16[1,256,128]{2,1,0:T(8,128)(2,1)S(1)}, u32[]{:S(2)}, u32[]{:S(2)}) collective-permute-start(bf16[1,256,128]{2,1,0:T(8,128)(2,1)S(1)} %get-tuple-element.20), channel_id=1, source_target_pairs={{0,1},{1,2},{2,3},{3,4},{4,5},{5,6},{6,7},{7,8},{8,9},{9,10},{10,1... | collective-permute-start | bytes 196616 | tf_op jit(solution)/shard_map/ppermute | solution.py:23
  356.3 5.9 %collective-permute-done.19 = bf16[1,256,128]{2,1,0:T(8,128)(2,1)S(1)} collective-permute-done((bf16[1,256,128]{2,1,0:T(8,128)(2,1)S(1)}, bf16[1,256,128]{2,1,0:T(8,128)(2,1)S(1)}, u32[]{:S(2)}, u32[]{:S(2)}) %collective-permute-start.19) | collective-permute-done | bytes 65568 | tf_op jit(solution)/shard_map/ppermute | solution.py:26
  368.9 3.2 fusion.1
  372.1 9.8 %all-to-all-start.1 = ((bf16[16,8,16384]{2,1,0:T(8,128)(2,1)}), bf16[16,8,16384]{2,1,0:T(8,128)(2,1)}, u32[]{:S(2)}, u32[]{:S(2)}) async-start(bf16[16,8,16384]{2,1,0:T(8,128)(2,1)} %fusion.1), calls=%async_computation.1 | async-start | bytes 8388608 | tf_op jit(solution)/shard_map/all_to_all | solution.py:307
  382.5 46.5 %all-to-all-done.1 = bf16[16,8,16384]{2,1,0:T(8,128)(2,1)} async-done(((bf16[16,8,16384]{2,1,0:T(8,128)(2,1)}), bf16[16,8,16384]{2,1,0:T(8,128)(2,1)}, u32[]{:S(2)}, u32[]{:S(2)}) %all-to-all-start.1) | async-done | bytes 4194336 | tf_op jit(solution)/shard_map/all_to_all | solution.py:307
  441.4 49.7 %reduce-scatter.5.cloned.1.call-done = bf16[464,512]{1,0:T(8,128)(2,1)} async-done(((bf16[7424,512]{1,0:T(8,128)(2,1)}), bf16[464,512]{1,0:T(8,128)(2,1)}) %reduce-scatter.5.cloned.1.call-update) | async-done | bytes 475152 | tf_op jit(solution)/shard_map/reduce_scatter | solution.py:57
  (380 shorter events, 161.6 us)
Async XLA Ops:
  19.0 61.3 %all-to-all-start = ((bf16[16,8,16384]{2,1,0:T(8,128)(2,1)}), bf16[16,8,16384]{2,1,0:T(8,128)(2,1)}, u32[]{:S(2)}, u32[]{:S(2)}) async-start(bf16[16,8,16384]{2,1,0:T(8,128)(2,1)} %fusion), calls=%async_computation | async-start | bytes 8388608 | tf_op jit(solution)/shard_map/all_to_all | solution.py:184
  27.1 408.6 %reduce-scatter.3.cloned.1.call-start = ((), (), s32[]{:S(2)}) async-start(), calls=%async_computation.4 | async-start | bytes 3063808 | tf_op jit(solution)/shard_map/reduce_scatter | solution.py:57
  27.6 52.8 %copy-start.49 = (bf16[32,128]{1,0:T(8,128)(2,1)}, bf16[32,128]{1,0:T(8,128)(2,1)S(1)}, u32[]{:S(2)}) copy-start(bf16[32,128]{1,0:T(8,128)(2,1)S(1)} %convolution_convert_fusion.18) | copy-start | bytes 24580
  86.6 7.7 %collective-permute-start = (bf16[1,256,128]{2,1,0:T(8,128)(2,1)S(1)}, bf16[1,256,128]{2,1,0:T(8,128)(2,1)S(1)}, u32[]{:S(2)}, u32[]{:S(2)}) collective-permute-start(bf16[1,256,128]{2,1,0:T(8,128)(2,1)S(1)} %get-tuple-element.26), channel_id=1, source_target_pairs={{0,1},{1,2},{2,3},{3,4},{4,5},{5,6},{6,7},{7,8},{8,9},{9,10},{10,1... | collective-permute-start | bytes 196616 | tf_op jit(solution)/shard_map/ppermute | solution.py:23
  92.1 6.2 %collective-permute-start.1 = (bf16[1,256,128]{2,1,0:T(8,128)(2,1)S(1)}, bf16[1,256,128]{2,1,0:T(8,128)(2,1)S(1)}, u32[]{:S(2)}, u32[]{:S(2)}) collective-permute-start(bf16[1,256,128]{2,1,0:T(8,128)(2,1)S(1)} %get-tuple-element.27), channel_id=1, source_target_pairs={{1,0},{2,1},{3,2},{4,3},{5,4},{6,5},{7,6},{8,7},{9,8},{10,9},{11,1... | collective-permute-start | bytes 196616 | tf_op jit(solution)/shard_map/ppermute | solution.py:26
  107.4 15.6 %copy-start.28 = (bf16[8,2,128,2,128]{2,0,4,3,1:T(8,128)(2,1)}, bf16[8,2,128,2,128]{2,0,4,3,1:T(8,128)(2,1)S(1)}, u32[]{:S(2)}) copy-start(bf16[8,2,128,2,128]{2,0,4,3,1:T(8,128)(2,1)S(1)} %copy.132) | copy-start | bytes 3145732
  107.9 8.5 %collective-permute-start.2 = (bf16[1,128,256]{2,1,0:T(8,128)(2,1)S(1)}, bf16[1,128,256]{2,1,0:T(8,128)(2,1)S(1)}, u32[]{:S(2)}, u32[]{:S(2)}) collective-permute-start(bf16[1,128,256]{2,1,0:T(8,128)(2,1)S(1)} %get-tuple-element.34), channel_id=1, source_target_pairs={{0,1},{1,2},{2,3},{3,4},{4,5},{5,6},{6,7},{7,8},{8,9},{9,10},{10,1... | collective-permute-start | bytes 196616 | tf_op jit(solution)/shard_map/ppermute | solution.py:23
  114.4 8.3 %collective-permute-start.3 = (bf16[1,128,256]{2,1,0:T(8,128)(2,1)S(1)}, bf16[1,128,256]{2,1,0:T(8,128)(2,1)S(1)}, u32[]{:S(2)}, u32[]{:S(2)}) collective-permute-start(bf16[1,128,256]{2,1,0:T(8,128)(2,1)S(1)} %get-tuple-element.35), channel_id=1, source_target_pairs={{1,0},{2,1},{3,2},{4,3},{5,4},{6,5},{7,6},{8,7},{9,8},{10,9},{11,1... | collective-permute-start | bytes 196616 | tf_op jit(solution)/shard_map/ppermute | solution.py:26
  129.2 8.8 %collective-permute-start.4 = (bf16[1,64,512]{2,1,0:T(8,128)(2,1)S(1)}, bf16[1,64,512]{2,1,0:T(8,128)(2,1)S(1)}, u32[]{:S(2)}, u32[]{:S(2)}) collective-permute-start(bf16[1,64,512]{2,1,0:T(8,128)(2,1)S(1)} %get-tuple-element.68), channel_id=1, source_target_pairs={{0,1},{1,2},{2,3},{3,4},{4,5},{5,6},{6,7},{7,8},{8,9},{9,10},{10,1... | collective-permute-start | bytes 196616 | tf_op jit(solution)/shard_map/ppermute | solution.py:23
  133.9 8.3 %collective-permute-start.5 = (bf16[1,64,512]{2,1,0:T(8,128)(2,1)S(1)}, bf16[1,64,512]{2,1,0:T(8,128)(2,1)S(1)}, u32[]{:S(2)}, u32[]{:S(2)}) collective-permute-start(bf16[1,64,512]{2,1,0:T(8,128)(2,1)S(1)} %get-tuple-element.69), channel_id=1, source_target_pairs={{1,0},{2,1},{3,2},{4,3},{5,4},{6,5},{7,6},{8,7},{9,8},{10,9},{11,1... | collective-permute-start | bytes 196616 | tf_op jit(solution)/shard_map/ppermute | solution.py:26
  148.0 8.9 %copy-start.41 = (bf16[256,512]{1,0:T(8,128)(2,1)S(1)}, bf16[256,512]{1,0:T(8,128)(2,1)}, u32[]{:S(2)}) copy-start(bf16[256,512]{1,0:T(8,128)(2,1)} %param.29) | copy-start | bytes 786436
  151.1 6.2 %collective-permute-start.6 = (bf16[1,128,256]{2,1,0:T(8,128)(2,1)S(1)}, bf16[1,128,256]{2,1,0:T(8,128)(2,1)S(1)}, u32[]{:S(2)}, u32[]{:S(2)}) collective-permute-start(bf16[1,128,256]{2,1,0:T(8,128)(2,1)S(1)} %get-tuple-element.32), channel_id=1, source_target_pairs={{0,1},{1,2},{2,3},{3,4},{4,5},{5,6},{6,7},{7,8},{8,9},{9,10},{10,1... | collective-permute-start | bytes 196616 | tf_op jit(solution)/shard_map/ppermute | solution.py:23
  155.0 8.1 %collective-permute-start.7 = (bf16[1,128,256]{2,1,0:T(8,128)(2,1)S(1)}, bf16[1,128,256]{2,1,0:T(8,128)(2,1)S(1)}, u32[]{:S(2)}, u32[]{:S(2)}) collective-permute-start(bf16[1,128,256]{2,1,0:T(8,128)(2,1)S(1)} %get-tuple-element.33), channel_id=1, source_target_pairs={{1,0},{2,1},{3,2},{4,3},{5,4},{6,5},{7,6},{8,7},{9,8},{10,9},{11,1... | collective-permute-start | bytes 196616 | tf_op jit(solution)/shard_map/ppermute | solution.py:26
  167.3 8.5 %slice-start.2 = ((s8[4718592]{0:T(1024)(128)(4,1)}), s8[4194304]{0:T(1024)(128)(4,1)S(1)}, s32[]{:S(2)}) async-start(s8[4718592]{0:T(1024)(128)(4,1)} %bitcast.279), calls=%async_computation.8 | async-start | bytes 8388608
  169.7 8.5 %collective-permute-start.8 = (bf16[1,256,128]{2,1,0:T(8,128)(2,1)S(1)}, bf16[1,256,128]{2,1,0:T(8,128)(2,1)S(1)}, u32[]{:S(2)}, u32[]{:S(2)}) collective-permute-start(bf16[1,256,128]{2,1,0:T(8,128)(2,1)S(1)} %get-tuple-element.24), channel_id=1, source_target_pairs={{0,1},{1,2},{2,3},{3,4},{4,5},{5,6},{6,7},{7,8},{8,9},{9,10},{10,1... | collective-permute-start | bytes 196616 | tf_op jit(solution)/shard_map/ppermute | solution.py:23
  173.6 6.3 %collective-permute-start.9 = (bf16[1,256,128]{2,1,0:T(8,128)(2,1)S(1)}, bf16[1,256,128]{2,1,0:T(8,128)(2,1)S(1)}, u32[]{:S(2)}, u32[]{:S(2)}) collective-permute-start(bf16[1,256,128]{2,1,0:T(8,128)(2,1)S(1)} %get-tuple-element.25), channel_id=1, source_target_pairs={{1,0},{2,1},{3,2},{4,3},{5,4},{6,5},{7,6},{8,7},{9,8},{10,9},{11,1... | collective-permute-start | bytes 196616 | tf_op jit(solution)/shard_map/ppermute | solution.py:26
  190.0 6.3 %collective-permute-start.10 = (bf16[1,256,128]{2,1,0:T(8,128)(2,1)S(1)}, bf16[1,256,128]{2,1,0:T(8,128)(2,1)S(1)}, u32[]{:S(2)}, u32[]{:S(2)}) collective-permute-start(bf16[1,256,128]{2,1,0:T(8,128)(2,1)S(1)} %get-tuple-element.22), channel_id=1, source_target_pairs={{0,1},{1,2},{2,3},{3,4},{4,5},{5,6},{6,7},{7,8},{8,9},{9,10},{10,1... | collective-permute-start | bytes 196616 | tf_op jit(solution)/shard_map/ppermute | solution.py:23
  194.0 6.3 %collective-permute-start.11 = (bf16[1,256,128]{2,1,0:T(8,128)(2,1)S(1)}, bf16[1,256,128]{2,1,0:T(8,128)(2,1)S(1)}, u32[]{:S(2)}, u32[]{:S(2)}) collective-permute-start(bf16[1,256,128]{2,1,0:T(8,128)(2,1)S(1)} %get-tuple-element.23), channel_id=1, source_target_pairs={{1,0},{2,1},{3,2},{4,3},{5,4},{6,5},{7,6},{8,7},{9,8},{10,9},{11,1... | collective-permute-start | bytes 196616 | tf_op jit(solution)/shard_map/ppermute | solution.py:26
  210.3 9.3 %collective-permute-start.12 = (bf16[1,128,256]{2,1,0:T(8,128)(2,1)S(1)}, bf16[1,128,256]{2,1,0:T(8,128)(2,1)S(1)}, u32[]{:S(2)}, u32[]{:S(2)}) collective-permute-start(bf16[1,128,256]{2,1,0:T(8,128)(2,1)S(1)} %get-tuple-element.30), channel_id=1, source_target_pairs={{0,1},{1,2},{2,3},{3,4},{4,5},{5,6},{6,7},{7,8},{8,9},{9,10},{10,1... | collective-permute-start | bytes 196616 | tf_op jit(solution)/shard_map/ppermute | solution.py:23
  214.2 6.7 %collective-permute-start.13 = (bf16[1,128,256]{2,1,0:T(8,128)(2,1)S(1)}, bf16[1,128,256]{2,1,0:T(8,128)(2,1)S(1)}, u32[]{:S(2)}, u32[]{:S(2)}) collective-permute-start(bf16[1,128,256]{2,1,0:T(8,128)(2,1)S(1)} %get-tuple-element.31), channel_id=1, source_target_pairs={{1,0},{2,1},{3,2},{4,3},{5,4},{6,5},{7,6},{8,7},{9,8},{10,9},{11,1... | collective-permute-start | bytes 196616 | tf_op jit(solution)/shard_map/ppermute | solution.py:26
  225.8 8.4 %copy-start.21 = (bf16[2304,256]{1,0:T(8,128)(2,1)S(1)}, bf16[2304,256]{1,0:T(8,128)(2,1)}, u32[]{:S(2)}) copy-start(bf16[2304,256]{1,0:T(8,128)(2,1)} %param.24) | copy-start | bytes 3538948
  227.9 16.4 %collective-permute-start.14 = (bf16[1,64,512]{2,1,0:T(8,128)(2,1)S(1)}, bf16[1,64,512]{2,1,0:T(8,128)(2,1)S(1)}, u32[]{:S(2)}, u32[]{:S(2)}) collective-permute-start(bf16[1,64,512]{2,1,0:T(8,128)(2,1)S(1)} %get-tuple-element.64), channel_id=1, source_target_pairs={{0,1},{1,2},{2,3},{3,4},{4,5},{5,6},{6,7},{7,8},{8,9},{9,10},{10,1... | collective-permute-start | bytes 196616 | tf_op jit(solution)/shard_map/ppermute | solution.py:23
  231.9 12.5 %collective-permute-start.15 = (bf16[1,64,512]{2,1,0:T(8,128)(2,1)S(1)}, bf16[1,64,512]{2,1,0:T(8,128)(2,1)S(1)}, u32[]{:S(2)}, u32[]{:S(2)}) collective-permute-start(bf16[1,64,512]{2,1,0:T(8,128)(2,1)S(1)} %get-tuple-element.65), channel_id=1, source_target_pairs={{1,0},{2,1},{3,2},{4,3},{5,4},{6,5},{7,6},{8,7},{9,8},{10,9},{11,1... | collective-permute-start | bytes 196616 | tf_op jit(solution)/shard_map/ppermute | solution.py:26
  258.2 9.6 %collective-permute-start.16 = (bf16[1,128,256]{2,1,0:T(8,128)(2,1)S(1)}, bf16[1,128,256]{2,1,0:T(8,128)(2,1)S(1)}, u32[]{:S(2)}, u32[]{:S(2)}) collective-permute-start(bf16[1,128,256]{2,1,0:T(8,128)(2,1)S(1)} %get-tuple-element.28), channel_id=1, source_target_pairs={{0,1},{1,2},{2,3},{3,4},{4,5},{5,6},{6,7},{7,8},{8,9},{9,10},{10,1... | collective-permute-start | bytes 196616 | tf_op jit(solution)/shard_map/ppermute | solution.py:23
  262.4 6.2 %collective-permute-start.17 = (bf16[1,128,256]{2,1,0:T(8,128)(2,1)S(1)}, bf16[1,128,256]{2,1,0:T(8,128)(2,1)S(1)}, u32[]{:S(2)}, u32[]{:S(2)}) collective-permute-start(bf16[1,128,256]{2,1,0:T(8,128)(2,1)S(1)} %get-tuple-element.29), channel_id=1, source_target_pairs={{1,0},{2,1},{3,2},{4,3},{5,4},{6,5},{7,6},{8,7},{9,8},{10,9},{11,1... | collective-permute-start | bytes 196616 | tf_op jit(solution)/shard_map/ppermute | solution.py:26
  265.1 9.9 %slice-start.4 = ((s8[9437184]{0:T(1024)(128)(4,1)}), s8[4194304]{0:T(1024)(128)(4,1)S(1)}, s32[]{:S(2)}) async-start(s8[9437184]{0:T(1024)(128)(4,1)} %bitcast.325), calls=%async_computation.10 | async-start | bytes 8388608
  293.9 197.2 %reduce-scatter.5.cloned.1.call-start = ((), (), s32[]{:S(2)}) async-start(), calls=%async_computation.5 | async-start | bytes 8077312 | tf_op jit(solution)/shard_map/reduce_scatter | solution.py:57
  348.4 7.9 %collective-permute-start.18 = (bf16[1,256,128]{2,1,0:T(8,128)(2,1)S(1)}, bf16[1,256,128]{2,1,0:T(8,128)(2,1)S(1)}, u32[]{:S(2)}, u32[]{:S(2)}) collective-permute-start(bf16[1,256,128]{2,1,0:T(8,128)(2,1)S(1)} %get-tuple-element.20), channel_id=1, source_target_pairs={{0,1},{1,2},{2,3},{3,4},{4,5},{5,6},{6,7},{7,8},{8,9},{9,10},{10,1... | collective-permute-start | bytes 196616 | tf_op jit(solution)/shard_map/ppermute | solution.py:23
  353.9 8.3 %collective-permute-start.19 = (bf16[1,256,128]{2,1,0:T(8,128)(2,1)S(1)}, bf16[1,256,128]{2,1,0:T(8,128)(2,1)S(1)}, u32[]{:S(2)}, u32[]{:S(2)}) collective-permute-start(bf16[1,256,128]{2,1,0:T(8,128)(2,1)S(1)} %get-tuple-element.21), channel_id=1, source_target_pairs={{1,0},{2,1},{3,2},{4,3},{5,4},{6,5},{7,6},{8,7},{9,8},{10,9},{11,1... | collective-permute-start | bytes 196616 | tf_op jit(solution)/shard_map/ppermute | solution.py:26
  372.1 56.9 %copy-start.53 = (s32[64]{0:T(128)S(1)}, s32[64]{0:T(128)}, u32[]{:S(2)}) copy-start(s32[64]{0:T(128)} %copy-done.52) | copy-start | bytes 772
  372.1 56.9 %all-to-all-start.1 = ((bf16[16,8,16384]{2,1,0:T(8,128)(2,1)}), bf16[16,8,16384]{2,1,0:T(8,128)(2,1)}, u32[]{:S(2)}, u32[]{:S(2)}) async-start(bf16[16,8,16384]{2,1,0:T(8,128)(2,1)} %fusion.1), calls=%async_computation.1 | async-start | bytes 8388608 | tf_op jit(solution)/shard_map/all_to_all | solution.py:307
  432.6 67.3 %copy-start.1 = (bf16[64,128,128]{2,1,0:T(8,128)(2,1)S(1)}, bf16[64,128,128]{2,1,0:T(8,128)(2,1)}, u32[]{:S(2)}) copy-start(bf16[64,128,128]{2,1,0:T(8,128)(2,1)} %param.16) | copy-start | bytes 6291460
  (56 other events, 170.1 us)
Sparse Core Ops, SparseCore 0:
  294.0 85.7 reduce-scatter.2
  383.3 107.7 reduce-scatter.4

commit v2 on v0

v2 whole, which is shorter than its diff:
```python
import functools

import jax
import jax.numpy as jnp
from jax import lax
from jax.experimental import pallas as pl
from jax.experimental.pallas import tpu as pltpu
from jax.sharding import PartitionSpec as P

BLK_DEV = 64
C1 = 256
C2 = 512
K = 128
TILE = 128
CAP = 8
MESH = pl.DeviceIdType.MESH


loss_weight = 0.0625


def flipped(weight):
    inward = weight.shape[0] // 9
    return weight.reshape(9, inward, -1)[::-1].transpose(0, 2, 1).reshape(-1, inward)


def silu_slope(signal):
    logistic = jax.nn.sigmoid(signal)
    return logistic * (1.0 + signal * (1.0 - logistic))


def outer(former, latter):
    return lax.dot_general(
        former, latter, (((0,), (0,)), ((), ())), preferred_element_type=jnp.float32
    )


def backward(former, latter):
    return lax.dot_general(
        former, latter, (((1,), (1,)), ((), ())), preferred_element_type=jnp.float32
    )


def lower_rows(block):
    moved = pltpu.roll(block.astype(jnp.float32), 1, 0)
    place = lax.broadcasted_iota(jnp.int32, moved.shape, 0)
    return jnp.where(place == 0, 0.0, moved).astype(block.dtype)


def upper_rows(block):
    length = block.shape[0]
    moved = pltpu.roll(block.astype(jnp.float32), length - 1, 0)
    place = lax.broadcasted_iota(jnp.int32, moved.shape, 0)
    return jnp.where(place == length - 1, 0.0, moved).astype(block.dtype)


def shifted_pair(row):
    span = 64
    blocks = [row[at : at + span] for at in range(0, row.shape[0], span)]
    if len(blocks) == 1:
        return lower_rows(row), upper_rows(row)
    if len(blocks) == 2:
        left = [lower_rows(blocks[1]), blocks[0]]
        right = [blocks[1], upper_rows(blocks[0])]
    else:
        left = [lower_rows(blocks[3]), blocks[2], blocks[0], blocks[1]]
        right = [blocks[2], blocks[3], blocks[1], upper_rows(blocks[0])]
    return jnp.concatenate(left, axis=0), jnp.concatenate(right, axis=0)


def window(start, size):
    if isinstance(start, int):
        return pl.ds(start, size)
    return pl.ds(pl.multiple_of(start, size if size < 64 else 64), size)


def put_row(field, at, row):
    span, channels = row.shape
    left, right = shifted_pair(row)
    rows = window(at * span, span)
    field[rows, 0:channels] = left
    field[rows, channels : 2 * channels] = row
    field[rows, 2 * channels : 3 * channels] = right


def tap_rows(field, first, count, span):
    return jnp.concatenate(
        [field[window((first + step) * span, count * span), :] for step in range(3)], axis=1
    )


def times(former, latter):
    return jnp.dot(former, latter, preferred_element_type=jnp.float32)


def unet_kernel(*refs):
    (
        zero_ref, labels_ref, fine_conv, fine_down, middle_conv, middle_down, coarse_conv,
        coarse_up, middle_merge, middle_up, fine_merge, head, flip_fine, flip_middle,
        flip_coarse, flip_merge, flip_top,
        zero_grad, loss_ref, g_fine, g_fine_down, g_middle, g_middle_down, g_coarse,
        g_coarse_up, g_merge, g_up, g_top, g_head,
        field_zero, field_top, field_fine, field_one, field_merge, field_middle, field_two,
        field_coarse, pre_fine, hid_fine, pre_middle, hid_middle, pre_coarse, hid_coarse,
        pre_merge, out_middle, grad_fine, grad_middle, grad_one, sum_fine, sum_middle, sum_head,
        edges_fine, edges_middle, edges_coarse, halo_fine, halo_middle, halo_coarse,
        send_sem, receive_sem,
    ) = refs
    bfloat, single = jnp.bfloat16, jnp.float32
    slab = lax.axis_index("slab")
    last = lax.axis_size("slab") - 1
    barrier = pltpu.get_barrier_semaphore()

    for step in (1, last):
        pl.semaphore_signal(
            barrier,
            inc=1,
            device_id={"slab": lax.rem(slab + step, last + 1)},
            device_id_type=MESH,
        )
    pl.semaphore_wait(barrier, 2)

    def edge_copy(source, halo, exchange, slot, way):
        return pltpu.make_async_remote_copy(
            src_ref=source,
            dst_ref=halo.at[slot, way],
            send_sem=send_sem.at[exchange, way],
            recv_sem=receive_sem.at[exchange, way],
            device_id={"slab": slab + (1 if way == 0 else -1)},
            device_id_type=MESH,
        )

    started = []

    def send_edges(top, bottom, halo, exchange, slot):
        started.append((top, bottom, halo, exchange, slot))

        @pl.when(slab < last)
        def _():
            edge_copy(bottom, halo, exchange, slot, 0).start()

        @pl.when(slab > 0)
        def _():
            edge_copy(top, halo, exchange, slot, 1).start()

    def take_edges(field, height):
        top, bottom, halo, exchange, slot = started[-1]

        @pl.when(slab > 0)
        def _():
            edge_copy(bottom, halo, exchange, slot, 0).wait_recv()

        @pl.when(slab == 0)
        def _():
            halo[slot, 0] = jnp.zeros(halo.shape[2:], halo.dtype)

        @pl.when(slab < last)
        def _():
            edge_copy(top, halo, exchange, slot, 1).wait_recv()

        @pl.when(slab == last)
        def _():
            halo[slot, 1] = jnp.zeros(halo.shape[2:], halo.dtype)

        put_row(field, 0, halo[slot, 0])
        put_row(field, height + 1, halo[slot, 1])

    def each(first, bound, body):
        def step(index, carry):
            body(index)
            return carry

        lax.fori_loop(first, bound, step, 0)

    def fine_rows(handle, inner, outer_):
        if inner:
            each(1, 7, handle)
        if outer_:
            each(0, 2, lambda index: handle(index * 7))

    def middle_rows(handle, inner, outer_):
        if inner:
            each(1, 3, handle)
        if outer_:
            each(0, 2, lambda index: handle(index * 3))

    quads = [(0, 0), (0, 1), (1, 0), (1, 1)]

    send_edges(zero_ref.at[0], zero_ref.at[15], halo_fine, 0, 0)
    each(0, 16, lambda row: put_row(field_zero, row + 1, zero_ref[row]))

    def fine_step(at):
        pre = times(tap_rows(field_zero, 2 * at, 2, 256), fine_conv[...])
        rows = window(at * 128, 128)
        for k in range(4):
            part = pre[k * 128 : (k + 1) * 128]
            pre_fine[rows, k * 128 : (k + 1) * 128] = part
            hid_fine[rows, k * 128 : (k + 1) * 128] = jax.nn.silu(part).astype(bfloat)

    fine_rows(fine_step, True, False)
    take_edges(field_zero, 16)
    fine_rows(fine_step, False, True)

    def one_step(at):
        value = times(hid_fine[window(at * 256, 256), :], fine_down[...]).astype(bfloat)
        for k in range(2):
            put_row(field_one, 2 * at + k + 1, value[k * 128 : (k + 1) * 128])

    def middle_edges(field, slot):
        edges_middle[slot, 0] = field[pl.ds(128, 128), 256:512]
        edges_middle[slot, 1] = field[pl.ds(8 * 128, 128), 256:512]

    middle_rows(one_step, False, True)
    middle_edges(field_one, 0)
    send_edges(edges_middle.at[0, 0], edges_middle.at[0, 1], halo_middle, 1, 0)
    middle_rows(one_step, True, False)

    def middle_step(at):
        pre = times(tap_rows(field_one, 2 * at, 2, 128), middle_conv[...])
        rows = window(at * 64, 64)
        for k in range(4):
            part = pre[k * 64 : (k + 1) * 64]
            pre_middle[rows, k * 256 : (k + 1) * 256] = part
            hid_middle[rows, k * 256 : (k + 1) * 256] = jax.nn.silu(part).astype(bfloat)

    middle_rows(middle_step, True, False)
    take_edges(field_one, 8)
    middle_rows(middle_step, False, True)

    def spread_coarse(field, value, slot, exchange):
        for row in range(4):
            put_row(field, row + 1, value[row * 64 : (row + 1) * 64])
        edges_coarse[slot, 0] = value[0:64]
        edges_coarse[slot, 1] = value[192:256]
        send_edges(edges_coarse.at[slot, 0], edges_coarse.at[slot, 1], halo_coarse, exchange, slot)

    def coarse_part(field, weight, step):
        return times(
            field[window(step * 64, 256), :], weight[window(step * 1536, 1536), :]
        )

    value = times(hid_middle[...], middle_down[...]).astype(bfloat)
    spread_coarse(field_two, value, 0, 2)
    pre_coarse[...] = coarse_part(field_two, coarse_conv, 1)
    take_edges(field_two, 4)

    def coarse_step(index):
        pre_coarse[...] += coarse_part(field_two, coarse_conv, 2 * index)

    each(0, 2, coarse_step)
    hid_coarse[...] = jax.nn.silu(pre_coarse[...]).astype(bfloat)

    def join_middle(at):
        rows = window(at * 64, 64)
        total = times(hid_coarse[rows, :], coarse_up[...]) + hid_middle[rows, :].astype(single)
        total = total.astype(bfloat)
        for i in range(2):
            row = jnp.concatenate(
                [total[:, (2 * i + j) * 256 : (2 * i + j + 1) * 256] for j in range(2)], axis=0
            )
            put_row(field_merge, 2 * at + i + 1, row)

    middle_rows(join_middle, False, True)
    middle_edges(field_merge, 1)
    send_edges(edges_middle.at[1, 0], edges_middle.at[1, 1], halo_middle, 3, 1)
    middle_rows(join_middle, True, False)

    def merge_step(at):
        pre = times(tap_rows(field_merge, 2 * at, 2, 128), middle_merge[...])
        rows = window(at * 256, 256)
        pre_merge[rows, :] = pre
        out_middle[rows, :] = jax.nn.silu(pre).astype(bfloat)

    middle_rows(merge_step, True, False)
    take_edges(field_merge, 8)
    middle_rows(merge_step, False, True)

    def join_fine(at):
        rows = window(at * 128, 128)
        total = times(out_middle[rows, :], middle_up[...]) + hid_fine[rows, :].astype(single)
        total = total.astype(bfloat)
        for i in range(2):
            row = jnp.concatenate(
                [total[:, (2 * i + j) * 128 : (2 * i + j + 1) * 128] for j in range(2)], axis=0
            )
            put_row(field_top, 2 * at + i + 1, row)

    def fine_edges(field, slot):
        edges_fine[slot, 0] = field[pl.ds(256, 256), 128:256]
        edges_fine[slot, 1] = field[pl.ds(16 * 256, 256), 128:256]

    fine_rows(join_fine, False, True)
    fine_edges(field_top, 0)
    send_edges(edges_fine.at[0, 0], edges_fine.at[0, 1], halo_fine, 4, 1)
    fine_rows(join_fine, True, False)
    sum_head[...] = jnp.zeros_like(sum_head)

    def top_step(at):
        pre = times(tap_rows(field_top, 2 * at, 2, 256), fine_merge[...])
        logistic = jax.nn.sigmoid(pre)
        out_fine = (pre * logistic).astype(bfloat)
        logits = times(out_fine, head[...])
        for i in range(2):
            row = logits[i * 256 : (i + 1) * 256]
            labels = labels_ref[2 * at + i].astype(single)
            spread = jnp.maximum(row, 0.0) + jnp.log1p(jnp.exp(-jnp.abs(row)))
            penalty = jnp.sum(spread - labels * row, axis=0, keepdims=True)
            loss_ref[2 * at + i] = jnp.broadcast_to(penalty, (8, 128))
            slope = ((jax.nn.sigmoid(row) - labels) * loss_weight).astype(bfloat)
            one = slice(i * 256, (i + 1) * 256)
            sum_head[...] += outer(out_fine[one], slope)
            level = logistic[one]
            down = backward(slope, head[...]) * (level * (1.0 + pre[one] * (1.0 - level)))
            put_row(field_fine, 2 * at + i + 1, down.astype(bfloat))

    fine_rows(top_step, True, False)
    take_edges(field_top, 16)
    fine_rows(top_step, False, True)
    g_head[...] = sum_head[...].astype(bfloat)
    fine_edges(field_fine, 1)
    send_edges(edges_fine.at[1, 0], edges_fine.at[1, 1], halo_fine, 5, 2)

    def fine_weight(field, grad_out):
        sum_fine[...] = jnp.zeros_like(sum_fine)

        def step(at):
            back = field_fine[window((2 * at + 1) * 256, 512), 128:256]
            sum_fine[...] += outer(back, tap_rows(field, 2 * at, 2, 256))

        each(0, 8, step)
        for k in range(9):
            part = sum_fine[:, k * 128 : (k + 1) * 128]
            grad_out[pl.ds(k * 128, 128), :] = part.T.astype(bfloat)

    fine_weight(field_top, g_top)
    take_edges(field_fine, 16)

    def grad_fine_step(at):
        value = times(tap_rows(field_fine, 2 * at, 2, 256), flip_top[...]).astype(bfloat)
        rows = window(at * 128, 128)
        for k in range(4):
            grad_fine[rows, k * 128 : (k + 1) * 128] = value[k * 128 : (k + 1) * 128]

    each(0, 8, grad_fine_step)

    def back_merge_step(at):
        rows = window(at * 256, 256)
        value = backward(grad_fine[rows, :], middle_up[...]) * silu_slope(pre_merge[rows, :])
        value = value.astype(bfloat)
        for k in range(2):
            put_row(field_middle, 2 * at + k + 1, value[k * 128 : (k + 1) * 128])

    each(0, 4, back_merge_step)
    middle_edges(field_middle, 2)
    send_edges(edges_middle.at[2, 0], edges_middle.at[2, 1], halo_middle, 6, 2)
    g_up[...] = outer(out_middle[...], grad_fine[...]).astype(bfloat)

    def middle_weight(field, grad_out):
        for part in range(3):
            total = jnp.zeros((256, 768), single)
            back = field_middle[pl.ds(128, 1024), 256:512]
            taps = field[pl.ds(part * 128, 1024), :]
            total = outer(back, taps)
            for k in range(3):
                grad_out[pl.ds(part * 768 + k * 256, 256), :] = (
                    total[:, k * 256 : (k + 1) * 256].T.astype(bfloat)
                )

    middle_weight(field_merge, g_merge)
    take_edges(field_middle, 8)

    def grad_middle_step(at):
        value = times(tap_rows(field_middle, 2 * at, 2, 128), flip_merge[...]).astype(bfloat)
        rows = window(at * 64, 64)
        for k in range(4):
            grad_middle[rows, k * 256 : (k + 1) * 256] = value[k * 64 : (k + 1) * 64]

    each(0, 4, grad_middle_step)

    value = backward(grad_middle[...], coarse_up[...]) * silu_slope(pre_coarse[...])
    spread_coarse(field_coarse, value.astype(bfloat), 1, 7)
    g_coarse_up[...] = outer(hid_coarse[...], grad_middle[...]).astype(bfloat)

    def coarse_weight(step):
        back = field_coarse[pl.ds(64, 256), 512:1024]
        total = outer(field_two[window(step * 64, 256), :], back)
        g_coarse[window(step * 1536, 1536), :] = total.astype(bfloat)

    each(0, 3, coarse_weight)
    take_edges(field_coarse, 4)
    pre_coarse[...] = coarse_part(field_coarse, flip_coarse, 1)

    def coarse_back(index):
        pre_coarse[...] += coarse_part(field_coarse, flip_coarse, 2 * index)

    each(0, 2, coarse_back)
    value = pre_coarse[...].astype(bfloat)

    hid_coarse[...] = value

    def back_middle_step(at):
        rows = window(at * 64, 64)
        total = backward(hid_coarse[rows, :], middle_down[...]) + grad_middle[rows, :].astype(single)
        total = (total * silu_slope(pre_middle[rows, :])).astype(bfloat)
        for i in range(2):
            row = jnp.concatenate(
                [total[:, (2 * i + j) * 256 : (2 * i + j + 1) * 256] for j in range(2)], axis=0
            )
            put_row(field_middle, 2 * at + i + 1, row)

    each(0, 4, back_middle_step)
    middle_edges(field_middle, 3)
    send_edges(edges_middle.at[3, 0], edges_middle.at[3, 1], halo_middle, 8, 3)
    g_middle_down[...] = outer(hid_middle[...], hid_coarse[...]).astype(bfloat)
    middle_weight(field_one, g_middle)
    take_edges(field_middle, 8)

    def grad_one_step(at):
        value = times(tap_rows(field_middle, 2 * at, 2, 128), flip_middle[...]).astype(bfloat)
        grad_one[window(at * 256, 256), :] = value

    each(0, 4, grad_one_step)

    def back_fine_step(at):
        rows = window(at * 128, 128)
        total = backward(grad_one[rows, :], fine_down[...]) + grad_fine[rows, :].astype(single)
        total = (total * silu_slope(pre_fine[rows, :])).astype(bfloat)
        for i in range(2):
            row = jnp.concatenate(
                [total[:, (2 * i + j) * 128 : (2 * i + j + 1) * 128] for j in range(2)], axis=0
            )
            put_row(field_fine, 2 * at + i + 1, row)

    each(0, 8, back_fine_step)
    fine_edges(field_fine, 2)
    send_edges(edges_fine.at[2, 0], edges_fine.at[2, 1], halo_fine, 9, 3)
    g_fine_down[...] = outer(hid_fine[...], grad_one[...]).astype(bfloat)
    fine_weight(field_zero, g_fine)
    take_edges(field_fine, 16)

    def zero_step(at):
        value = times(tap_rows(field_fine, 2 * at, 2, 256), flip_fine[...]).astype(bfloat)
        for i in range(2):
            zero_grad[2 * at + i] = value[i * 256 : (i + 1) * 256]

    each(0, 8, zero_step)

    for top, bottom, halo, exchange, slot in started:

        @pl.when(slab < last)
        def _():
            edge_copy(bottom, halo, exchange, slot, 0).wait_send()

        @pl.when(slab > 0)
        def _():
            edge_copy(top, halo, exchange, slot, 1).wait_send()


def unet(*operands):
    bfloat, single = jnp.bfloat16, jnp.float32
    shapes = [
        ((16, 256, 128), bfloat), ((16, 8, 128), single), ((1152, 128), bfloat),
        ((512, 256), bfloat), ((2304, 256), bfloat), ((1024, 512), bfloat),
        ((4608, 512), bfloat), ((512, 1024), bfloat), ((2304, 256), bfloat),
        ((256, 512), bfloat), ((1152, 128), bfloat), ((128, 128), bfloat),
    ]
    scratch = [
        ((18 * 256, 384), bfloat), ((18 * 256, 384), bfloat), ((18 * 256, 384), bfloat),
        ((10 * 128, 768), bfloat), ((10 * 128, 768), bfloat), ((10 * 128, 768), bfloat),
        ((6 * 64, 1536), bfloat), ((6 * 64, 1536), bfloat),
        ((1024, 512), single), ((1024, 512), bfloat),
        ((256, 1024), single), ((256, 1024), bfloat),
        ((256, 512), single), ((256, 512), bfloat),
        ((1024, 256), single), ((1024, 256), bfloat),
        ((1024, 512), bfloat), ((256, 1024), bfloat), ((1024, 256), bfloat),
        ((128, 1152), single), ((8, 128), single), ((128, 128), single),
        ((3, 2, 256, 128), bfloat), ((4, 2, 128, 256), bfloat), ((2, 2, 64, 512), bfloat),
        ((4, 2, 256, 128), bfloat), ((4, 2, 128, 256), bfloat), ((2, 2, 64, 512), bfloat),
    ]
    return pl.pallas_call(
        unet_kernel,
        out_shape=[jax.ShapeDtypeStruct(*leaf) for leaf in shapes],
        in_specs=[pl.BlockSpec(memory_space=pltpu.VMEM)] * len(operands),
        out_specs=[pl.BlockSpec(memory_space=pltpu.VMEM)] * len(shapes),
        scratch_shapes=[pltpu.VMEM(*leaf) for leaf in scratch]
        + [pltpu.SemaphoreType.DMA((10, 2)), pltpu.SemaphoreType.DMA((10, 2))],
        compiler_params=pltpu.CompilerParams(
            collective_id=0, has_side_effects=True, vmem_limit_bytes=67043328
        ),
        cost_estimate=pl.CostEstimate(
            flops=24_000_000_000, bytes_accessed=40_000_000, transcendentals=4_000_000
        ),
    )(*operands)


def scatter_jobs(shapes):
    order = [(4, 0, 96), (6, 0, None), (2, 0, None), (4, 96, 96), (3, 0, None), (5, 0, None)]
    order += [(4, 192, 96)] + [(at, 0, None) for at in (1, 7, 0, 8, 9)]
    return [(at, row, size or shapes[at][0], at == 4) for at, row, size in order]


def scatter_kernel(jobs, *refs):
    single = jnp.float32
    count = len(jobs)
    terms, refs = refs[:10], refs[10:]
    outs, refs = refs[:10], refs[10:]
    own, refs = refs[:count], refs[count:]
    landed, refs = refs[:count], refs[count:]
    partial, refs = refs[:count], refs[count:]
    final, refs = refs[:count], refs[count:]
    own_sem, send_one, receive_one, send_two, receive_two = refs
    slab = lax.axis_index("slab")
    y, z = slab // 4, slab % 4
    barrier = pltpu.get_barrier_semaphore()

    def peer(along_y, step):
        if along_y:
            spot = (y + step) % 4
            return spot, spot * 4 + z
        spot = (z + step) % 4
        return spot, y * 4 + spot

    for along_y in (True, False):
        for step in (1, 2, 3):
            pl.semaphore_signal(
                barrier,
                inc=1,
                device_id={"slab": peer(along_y, step)[1]},
                device_id_type=MESH,
            )
    pl.semaphore_wait(barrier, 6)

    def group(job, spot):
        at, row, size, along_y = jobs[job]
        rows = pl.ds(row, size)
        if along_y:
            return terms[at].at[spot, :, rows]
        return terms[at].at[:, spot, rows]

    def keep(job):
        return pltpu.make_async_copy(
            group(job, y if jobs[job][3] else z), own[job], own_sem.at[job]
        )

    def first(job, step):
        spot, target = peer(jobs[job][3], step)
        return pltpu.make_async_remote_copy(
            src_ref=group(job, spot),
            dst_ref=landed[job].at[step - 1],
            send_sem=send_one.at[job, step - 1],
            recv_sem=receive_one.at[job, step - 1],
            device_id={"slab": target},
            device_id_type=MESH,
        )

    def second(job, step):
        spot, target = peer(not jobs[job][3], step)
        return pltpu.make_async_remote_copy(
            src_ref=partial[job].at[spot],
            dst_ref=final[job].at[step - 1],
            send_sem=send_two.at[job, step - 1],
            recv_sem=receive_two.at[job, step - 1],
            device_id={"slab": target},
            device_id_type=MESH,
        )

    for job in range(count):
        for step in (2, 1, 3):
            first(job, step).start()
        keep(job).start()
    for job in range(count):
        keep(job).wait()
        for step in (1, 2, 3):
            first(job, step).wait_recv()

        def add(spot, carry, job=job):
            total = own[job][spot].astype(single)
            for step in range(3):
                total = total + landed[job][step, spot].astype(single)
            partial[job][spot] = total.astype(jnp.bfloat16)
            return carry

        lax.fori_loop(0, 4, add, 0)
        for step in (2, 1, 3):
            second(job, step).start()
    for job in range(count):
        at, row, size, along_y = jobs[job]
        for step in (1, 2, 3):
            second(job, step).wait_recv()
        total = partial[job][z if along_y else y].astype(single)
        for step in range(3):
            total = total + final[job][step].astype(single)
        outs[at][pl.ds(row, size), :] = total
    for job in range(count):
        for step in (1, 2, 3):
            first(job, step).wait_send()
            second(job, step).wait_send()


def scatter_sums(terms):
    bfloat = jnp.bfloat16
    shapes = [(term.shape[0] // 16, term.shape[1]) for term in terms]
    jobs = scatter_jobs(shapes)
    blocks = [(size, shapes[at][1]) for at, _, size, _ in jobs]
    scratch = [pltpu.VMEM((4, *block), bfloat) for block in blocks]
    scratch += [pltpu.VMEM((3, 4, *block), bfloat) for block in blocks]
    scratch += [pltpu.VMEM((4, *block), bfloat) for block in blocks]
    scratch += [pltpu.VMEM((3, *block), bfloat) for block in blocks]
    scratch += [pltpu.SemaphoreType.DMA((len(jobs),))]
    scratch += [pltpu.SemaphoreType.DMA((len(jobs), 3)) for _ in range(4)]
    return pl.pallas_call(
        functools.partial(scatter_kernel, jobs),
        out_shape=[jax.ShapeDtypeStruct(shape, jnp.float32) for shape in shapes],
        in_specs=[pl.BlockSpec(memory_space=pl.ANY)] * len(terms),
        out_specs=[pl.BlockSpec(memory_space=pltpu.VMEM)] * len(terms),
        scratch_shapes=scratch,
        compiler_params=pltpu.CompilerParams(
            collective_id=1, has_side_effects=True, vmem_limit_bytes=40000000
        ),
        cost_estimate=pl.CostEstimate(
            flops=2_000_000_000, bytes_accessed=30_000_000, transcendentals=0
        ),
    )(*[term.reshape(4, 4, *shape) for term, shape in zip(terms, shapes)])


def by_parity(field):
    rows, across, channels = field.shape
    return (
        field.reshape(rows, across // 4, 2, 2, channels)
        .transpose(0, 3, 2, 1, 4)
        .reshape(rows, across, channels)
    )


def body(
    camera_features,
    cell_index,
    owner_device,
    owner_tile,
    base_map,
    targets,
    fine_conv,
    fine_down,
    middle_conv,
    middle_down,
    coarse_conv,
    coarse_up,
    middle_merge,
    middle_up,
    fine_merge,
    head_weight,
):
    single = jnp.float32
    bfloat = jnp.bfloat16
    device = lax.axis_index("slab")
    devices = lax.axis_size("slab")
    height, across, channels = base_map.shape
    slot_count = devices * CAP
    tile_count = height * across // TILE
    owners = owner_device[:, 0]
    everyone = owners.shape[0]
    choose = (owners[:, None] == jnp.arange(devices, dtype=jnp.int32)[None, :]).astype(jnp.int32)
    grouped = choose.reshape(devices, BLK_DEV, devices)
    earlier = (jnp.cumsum(grouped, axis=1) - grouped).reshape(everyone, devices)
    ranking = jnp.sum(earlier * choose, axis=1)
    sources = jnp.arange(everyone, dtype=jnp.int32) // BLK_DEV
    slot_number = owners * CAP + ranking
    local_slot = lax.dynamic_slice_in_dim(slot_number, device * BLK_DEV, BLK_DEV)
    slot_range = jnp.arange(slot_count, dtype=jnp.int32)
    send_map = (local_slot[None, :] == slot_range[:, None]).astype(bfloat)
    arrival = sources * CAP + ranking
    receive_map = ((arrival[None, :] == slot_range[:, None]) & (owners[None, :] == device)).astype(
        jnp.int32
    )
    tile_onehot = (owner_tile[:, None] == jnp.arange(tile_count, dtype=jnp.int32)[None, :]).astype(
        jnp.int32
    )
    placement = jnp.einsum("bt,sb->ts", tile_onehot, receive_map).astype(bfloat)
    cell_range = jnp.arange(TILE, dtype=jnp.int32)
    local_cells = lax.dynamic_slice_in_dim(cell_index, device * BLK_DEV, BLK_DEV)
    local_cells = local_cells % 2 * 64 + local_cells // 2 % 2 * 32 + local_cells // 4
    cell_onehot = (local_cells[:, :, None] == cell_range[None, None, :]).astype(bfloat)
    payload = (
        jnp.einsum("bpt,bpc->btc", cell_onehot, camera_features, preferred_element_type=single)
        .astype(bfloat)
        .reshape(BLK_DEV, -1)
    )
    outgoing = (
        jnp.dot(send_map, payload, preferred_element_type=single)
        .astype(bfloat)
        .reshape(devices, CAP, -1)
    )
    incoming = lax.all_to_all(outgoing, "slab", split_axis=0, concat_axis=0, tiled=True).reshape(
        slot_count, -1
    )
    canvas = jnp.dot(placement, incoming, preferred_element_type=single)
    canvas = canvas.reshape(height, 2, 4, 32, channels).transpose(0, 2, 1, 3, 4)
    level_zero = (
        by_parity(base_map).astype(single) + canvas.reshape(height, across, channels)
    ).astype(bfloat)
    level_zero_grad, losses, *terms = unet(
        level_zero,
        by_parity(targets),
        fine_conv,
        fine_down,
        middle_conv,
        middle_down,
        coarse_conv,
        coarse_up,
        middle_merge,
        middle_up,
        fine_merge,
        head_weight,
        flipped(fine_conv),
        flipped(middle_conv),
        flipped(coarse_conv),
        flipped(middle_merge),
        flipped(fine_merge),
    )
    row_loss = jnp.sum(losses[:, 0, :], axis=1) / (across * K)
    level_zero_grad = level_zero_grad.reshape(height, 4, 2, 32, channels).transpose(0, 2, 1, 3, 4)
    tiles_grad = level_zero_grad.reshape(tile_count, -1)
    slot_grad = jnp.einsum(
        "ts,tl->sl", placement, tiles_grad, preferred_element_type=single
    ).astype(bfloat)
    returned = lax.all_to_all(
        slot_grad.reshape(devices, CAP, -1), "slab", split_axis=0, concat_axis=0, tiled=True
    ).reshape(slot_count, -1)
    own_blocks = jnp.einsum("sb,sl->bl", send_map, returned, preferred_element_type=single).astype(
        bfloat
    )
    camera_grad = jnp.einsum(
        "bpt,btc->bpc",
        cell_onehot,
        own_blocks.reshape(BLK_DEV, TILE, channels),
        preferred_element_type=single,
    ).astype(bfloat)
    sums = scatter_sums(terms)
    return (camera_grad, row_loss, *sums)


def solution(mesh):
    step = jax.shard_map(
        body,
        mesh=mesh,
        in_specs=(
            P(("scene", "slab"), None, None),
            P("scene", None),
            P("scene", None),
            P("scene"),
            P(("scene", "slab"), None, None),
            P(("scene", "slab"), None, None),
            P(),
            P(),
            P(),
            P(),
            P(),
            P(),
            P(),
            P(),
            P(),
            P(),
        ),
        out_specs=(
            P(("scene", "slab"), None, None),
            P(("scene", "slab")),
            P(("scene", "slab"), None),
            P(("scene", "slab"), None),
            P(("scene", "slab"), None),
            P(("scene", "slab"), None),
            P(("scene", "slab"), None),
            P(("scene", "slab"), None),
            P(("scene", "slab"), None),
            P(("scene", "slab"), None),
            P(("scene", "slab"), None),
            P(("scene", "slab"), None),
        ),
        check_vma=False,
    )
    return step
```

time: 574 us -> 340 us (0.59); the launches traced: 566 us -> 338 us
  waiting for transfers between devices: 266 us -> 34.1 us
  Pallas kernels: 0 us -> 207 us
  starting transfers between devices: 87.8 us -> 19.5 us
  matrix products: 85 us -> 20.8 us
  local copies, waits for them, and re-layouts: 89.1 us -> 49.7 us
  between operations: 17 us -> 0.94 us
  other arithmetic: 20.3 us -> 6.46 us
    pallas_call x0 -> x2, Pallas kernels: none -> 207 us  [the longest x1 111 us: scatter_sums(): pl.pallas_call(functools.partial(scatter_kernel, jobs), out_shape=[jax.Sh...]
    reduce_scatter x1 -> x0, waiting for transfers between devices: 72.8 us -> none  [body(): lax.psum_scatter(outer(taps_coarse, back_coarse).astype(jnp.bfloat16), 's...]
    unnamed x3 -> x0, waiting for transfers between devices: 68 us -> none
    ppermute x20 -> x0, starting transfers between devices: 66.5 us -> none  [the longest x10 45.9 us: extended(): lax.ppermute(lax.slice_in_dim(block, block.shape[dim] - width, None, axis...]
    dot_general x31 -> x1, matrix products: 68.7 us -> 3.71 us  [body(): canvas = jnp.dot(placement, incoming, preferred_element_type=single)]
    all_to_all x1, waiting for transfers between devices: 44.5 us -> 0.01 us  [body(): lax.all_to_all(slot_grad.reshape(devices, CAP, -1), 'slab', split_axis=0,...]
    ppermute x20 -> x0, waiting for transfers between devices: 28.4 us -> none  [the longest x10 28.4 us: extended(): lax.ppermute(lax.slice_in_dim(block, 0, width, axis=dim), axis, backward)]
    transpose x14 -> x1, local copies, waits for them, and re-layouts: 26.7 us -> 0.69 us  [body(): canvas = canvas.reshape(height, 2, 4, 32, channels).transpose(0, 2, 1, 3, 4)]
  transfers between devices with their start and end apart: 24 -> 2, of which waited for: 13 -> 1; matrix products, arithmetic and copies ran while one was open for 11% -> 6% of each run, Pallas kernels for 0% -> 33%
where the time goes in v2:
time: 340 us; the launch traced here: 338 us
  Pallas kernels  207 us (61%)
  local copies, waits for them, and re-layouts  49.7 us (15%)
  waiting for transfers between devices  34.1 us (10%)
  matrix products  20.8 us (6%)
  starting transfers between devices  19.5 us (6%)
  other arithmetic  6.46 us (2%)
    pallas_call x1, Pallas kernels, scatter_sums(): pl.pallas_call(functools.partial(scatter_kernel, jobs), out_shape=[jax.Sh...  111 us
    pallas_call x1, Pallas kernels, unet(): pl.pallas_call(unet_kernel, out_shape=[jax.ShapeDtypeStruct(*leaf) for le...  95.9 us
    all_to_all x1, waiting for transfers between devices, body(): lax.all_to_all(outgoing, 'slab', split_axis=0, concat_axis=0, tiled=True)  34.1 us
    unnamed x94, local copies, waits for them, and re-layouts  21.8 us
    all_to_all x1, starting transfers between devices, body(): lax.all_to_all(slot_grad.reshape(devices, CAP, -1), 'slab', split_axis=0,...  11.4 us
    reshape x5, local copies, waits for them, and re-layouts, flipped(): weight.reshape(9, inward, -1)[::-1].transpose(0, 2, 1).reshape(-1, inward)  8.55 us
    rev x5, local copies, waits for them, and re-layouts, flipped(): weight.reshape(9, inward, -1)[::-1].transpose(0, 2, 1).reshape(-1, inward)  8.53 us
    all_to_all x1, starting transfers between devices, body(): lax.all_to_all(outgoing, 'slab', split_axis=0, concat_axis=0, tiled=True)  8.08 us
  transfers between devices with their start and end apart: 2, of which 1 were waited for; matrix products, arithmetic and copies ran while one was open for 6% of the time, Pallas kernels for 33%

profile of v2, /device:TPU:46, one launch (start us, length us, event | category | flops | bytes accessed | tf_op | source)
XLA Modules:
  0.0 338.4 jit_solution(7736102978147619313)
XLA Ops:
  1.2 1.3 broadcast_multiply_fusion
  2.7 1.4 select_reduce_fusion
  4.3 0.8 fusion.29
  5.2 3.9 %fusion.10 = bf16[64,128,128]{2,1,0:T(8,128)(2,1)S(1)} fusion(bf16[64,128,128]{2,1,0:T(8,128)(2,1)} %param.16, s32[64,128]{1,0:T(8,128)S(1)} %fusion.29), kind=kOutput, calls=%fused_computation.15 | convolution fusion | flops 270532608 | bytes 4227072 | tf_op jit(solution)/shard_map/bpt,bpc->btc/dot_general | solution.py:684
  9.1 3.6 %fusion = bf16[16,8,16384]{2,1,0:T(8,128)(2,1)} fusion(bf16[8,8,128,128]{3,2,1,0:T(8,128)(2,1)S(1)} %bitcast.97, s32[64]{0:T(128)S(1)} %dynamic_slice.7), kind=kOutput, calls=%fused_computation.2 | convolution fusion | flops 270540800 | bytes 6291712 | tf_op jit(solution)/shard_map/dot_general | solution.py:689
  12.7 8.1 %all-to-all-start = ((bf16[16,8,16384]{2,1,0:T(8,128)(2,1)}), bf16[16,8,16384]{2,1,0:T(8,128)(2,1)}, u32[]{:S(2)}, u32[]{:S(2)}) async-start(bf16[16,8,16384]{2,1,0:T(8,128)(2,1)} %fusion), calls=%async_computation | async-start | bytes 8388608 | tf_op jit(solution)/shard_map/all_to_all | solution.py:693
  21.0 0.8 rev.19
  22.7 1.3 copy.73
  24.7 1.1 rev.18
  26.6 1.1 rev.16
  28.0 6.7 %copy.76 = bf16[9,512,512]{1,2,0:T(8,128)(2,1)} copy(bf16[9,512,512]{2,1,0:T(8,128)(2,1)} %bitcast.99) | data formatting | bytes 9437184 | tf_op jit(solution)/shard_map/reshape | solution.py:24
  34.6 4.8 %rev.17 = bf16[9,512,512]{1,2,0:T(8,128)(2,1)} reverse(bf16[9,512,512]{1,2,0:T(8,128)(2,1)} %copy.76), dimensions={0} | reverse | bytes 9437184 | tf_op jit(solution)/shard_map/rev | solution.py:24
  39.9 34.1 %all-to-all-done = bf16[16,8,16384]{2,1,0:T(8,128)(2,1)} async-done(((bf16[16,8,16384]{2,1,0:T(8,128)(2,1)}), bf16[16,8,16384]{2,1,0:T(8,128)(2,1)}, u32[]{:S(2)}, u32[]{:S(2)}) %all-to-all-start) | async-done | bytes 4194336 | tf_op jit(solution)/shard_map/all_to_all | solution.py:693
  74.0 6.4 %copy.70 = bf16[128,16384]{0,1:T(8,128)(2,1)} copy(bf16[128,16384]{1,0:T(8,128)(2,1)} %bitcast.7) | data formatting | bytes 8388608 | tf_op jit(solution)/shard_map/reshape | solution.py:693
  80.4 3.7 %convolution_bitcast_fusion = f32[16,4,2,32,128]{4,0,3,1,2:T(8,128)S(1)} fusion(bf16[4,32,128,128,1]{3,2,1,0,4:T(8,128)(2,1)} %bitcast.96, bf16[16,2,128,1,1]{2,1,0,4,3:T(2,128)(2,1)S(1)} %bitcast.114), kind=kOutput, calls=%fused_computation.18 | convolution fusion | flops 134217728 | bytes 6299648 | tf_op jit(solution)/shard_map/dot_general | solution.py:696
  84.8 1.3 fusion.7.refs_0_
  86.0 95.9 %shard_map.247 = (bf16[16,256,128]{2,1,0:T(8,128)(2,1)}, f32[16,8,128]{2,1,0:T(8,128)}, bf16[1152,128]{1,0:T(8,128)(2,1)}, bf16[512,256]{1,0:T(8,128)(2,1)}, bf1...) custom-call(bf16[16,256,128]{2,1,0:T(8,128)(2,1)} %fusion.7.refs_0_,, ...), custom_call_target="tpu_custom_call" | custom-call | flops 24000000000 | bytes 40000000 | tf_op jit(solution)/shard_map/pallas_call | solution.py:480
  181.9 1.4 copy.93
  183.8 3.3 fusion.1
  187.1 11.4 %all-to-all-start.1 = ((bf16[16,8,16384]{2,1,0:T(8,128)(2,1)}), bf16[16,8,16384]{2,1,0:T(8,128)(2,1)}, u32[]{:S(2)}, u32[]{:S(2)}) async-start(bf16[16,8,16384]{2,1,0:T(8,128)(2,1)} %fusion.1), calls=%async_computation.1 | async-start | bytes 8388608 | tf_op jit(solution)/shard_map/all_to_all | solution.py:726
  198.6 2.3 copy-done
  200.9 1.2 copy-done.4
  202.1 1.0 copy-done.7
  203.1 1.0 copy-done.8
  204.1 0.9 copy-done.9
  205.0 0.9 copy-done.10
  206.7 111.1 %shard_map.248 = (f32[72,128]{1,0:T(8,128)S(1)}, f32[32,256]{1,0:T(8,128)S(1)}, f32[144,256]{1,0:T(8,128)S(1)}, f32[64,512]{1,0:T(8,128)S(1)}, f32[288,512]{1,0:...) custom-call(bf16[4,4,72,128]{3,2,1,0:T(8,128)(2,1)S(1)} %bitcast.91,, ...), custom_call_target="tpu_custom_call" | custom-call | flops 2000000000 | bytes 30000000 | tf_op jit(solution)/shard_map/pallas_call | solution.py:611
  317.8 0.8 copy-done.5
  323.6 1.0 slice_reduce_fusion
  325.2 3.0 fusion.12
  328.9 3.0 fusion.11
  334.5 0.8 copy.108
  (104 shorter events, 18.2 us)
Async XLA Ops:
  4.3 4.8 %copy-start.39 = (s32[64]{0:T(128)}, s32[64]{0:T(128)S(1)}, u32[]{:S(2)}) copy-start(s32[64]{0:T(128)S(1)} %dynamic_slice.7) | copy-start | bytes 772
  5.2 3.9 %copy-start.32 = (s32[64,128]{1,0:T(8,128)}, s32[64,128]{1,0:T(8,128)S(1)}, u32[]{:S(2)}) copy-start(s32[64,128]{1,0:T(8,128)S(1)} %fusion.29) | copy-start | bytes 98308
  12.7 8.1 %copy-start.35 = (bf16[1152,128]{1,0:T(8,128)(2,1)S(1)}, bf16[1152,128]{1,0:T(8,128)(2,1)}, u32[]{:S(2)}) copy-start(bf16[1152,128]{1,0:T(8,128)(2,1)} %refs_10_.1) | copy-start | bytes 884740
  12.7 9.1 %copy-start.34 = (bf16[1152,128]{1,0:T(8,128)(2,1)S(1)}, bf16[1152,128]{1,0:T(8,128)(2,1)}, u32[]{:S(2)}) copy-start(bf16[1152,128]{1,0:T(8,128)(2,1)} %refs_2_.1) | copy-start | bytes 884740
  12.7 61.3 %all-to-all-start = ((bf16[16,8,16384]{2,1,0:T(8,128)(2,1)}), bf16[16,8,16384]{2,1,0:T(8,128)(2,1)}, u32[]{:S(2)}, u32[]{:S(2)}) async-start(bf16[16,8,16384]{2,1,0:T(8,128)(2,1)} %fusion), calls=%async_computation | async-start | bytes 8388608 | tf_op jit(solution)/shard_map/all_to_all | solution.py:693
  20.8 2.0 copy-start.31
  20.8 3.2 copy-start.29
  24.0 1.9 copy-start.28
  25.9 1.8 copy-start.30
  34.6 4.8 %copy-start.38 = (s32[1024,1]{0,1:T(1,128)S(1)}, s32[1024,1]{0,1:T(1,128)}, u32[]{:S(2)}) copy-start(s32[1024,1]{0,1:T(1,128)} %param.18) | copy-start | bytes 12292
  34.6 4.8 %copy-start.40 = (s32[1024]{0:T(1024)S(1)}, s32[1024]{0:T(1024)}, u32[]{:S(2)}) copy-start(s32[1024]{0:T(1024)} %param.19) | copy-start | bytes 12292
  39.9 40.5 %copy-start.36 = (bf16[32,128]{1,0:T(8,128)(2,1)}, bf16[32,128]{1,0:T(8,128)(2,1)S(1)}, u32[]{:S(2)}) copy-start(bf16[32,128]{1,0:T(8,128)(2,1)S(1)} %convolution_convert_fusion.3) | copy-start | bytes 24580
  181.9 1.9 copy-start.37
  187.1 11.4 %copy-start.1 = (bf16[2304,256]{1,0:T(8,128)(2,1)S(1)}, bf16[2304,256]{1,0:T(8,128)(2,1)}, u32[]{:S(2)}) copy-start(bf16[2304,256]{1,0:T(8,128)(2,1)} %get-tuple-element.38) | copy-start | bytes 3538948
  187.1 11.4 %copy-start.2 = (bf16[2304,256]{1,0:T(8,128)(2,1)S(1)}, bf16[2304,256]{1,0:T(8,128)(2,1)}, u32[]{:S(2)}) copy-start(bf16[2304,256]{1,0:T(8,128)(2,1)} %get-tuple-element.42) | copy-start | bytes 3538948
  187.1 11.4 %copy-start.3 = (bf16[1024,512]{1,0:T(8,128)(2,1)S(1)}, bf16[1024,512]{1,0:T(8,128)(2,1)}, u32[]{:S(2)}) copy-start(bf16[1024,512]{1,0:T(8,128)(2,1)} %get-tuple-element.39) | copy-start | bytes 3145732
  187.1 138.0 %all-to-all-start.1 = ((bf16[16,8,16384]{2,1,0:T(8,128)(2,1)}), bf16[16,8,16384]{2,1,0:T(8,128)(2,1)}, u32[]{:S(2)}, u32[]{:S(2)}) async-start(bf16[16,8,16384]{2,1,0:T(8,128)(2,1)} %fusion.1), calls=%async_computation.1 | async-start | bytes 8388608 | tf_op jit(solution)/shard_map/all_to_all | solution.py:726
  198.6 2.3 copy-start
  200.9 1.2 copy-start.4
  202.1 1.0 copy-start.7
  203.1 1.0 copy-start.8
  204.1 0.9 copy-start.9
  205.0 0.9 copy-start.10
  328.9 3.0 copy-start.20
  328.9 3.6 %copy-start.25 = (f32[32,256]{1,0:T(8,128)S(1)}, f32[32,256]{1,0:T(8,128)}, u32[]{:S(2)}) copy-start(f32[32,256]{1,0:T(8,128)} %copy-done.24) | copy-start | bytes 98308
  328.9 4.3 %copy-start.12 = (f32[144,256]{1,0:T(8,128)S(1)}, f32[144,256]{1,0:T(8,128)}, u32[]{:S(2)}) copy-start(f32[144,256]{1,0:T(8,128)} %copy-done.11) | copy-start | bytes 442372
  328.9 4.9 %copy-start.16 = (f32[64,512]{1,0:T(8,128)S(1)}, f32[64,512]{1,0:T(8,128)}, u32[]{:S(2)}) copy-start(f32[64,512]{1,0:T(8,128)} %copy-done.15) | copy-start | bytes 393220
  328.9 5.6 %copy-start.6 = (f32[288,512]{1,0:T(8,128)S(1)}, f32[288,512]{1,0:T(8,128)}, u32[]{:S(2)}) copy-start(f32[288,512]{1,0:T(8,128)} %copy-done.5) | copy-start | bytes 1769476
  328.9 6.4 %copy-start.14 = (f32[32,1024]{1,0:T(8,128)S(1)}, f32[32,1024]{1,0:T(8,128)}, u32[]{:S(2)}) copy-start(f32[32,1024]{1,0:T(8,128)} %copy-done.13) | copy-start | bytes 393220
  331.9 4.7 %copy-start.23 = (f32[16,512]{1,0:T(8,128)S(1)}, f32[16,512]{1,0:T(8,128)}, u32[]{:S(2)}) copy-start(f32[16,512]{1,0:T(8,128)} %copy-done.22) | copy-start | bytes 98308
  331.9 5.3 %copy-start.18 = (f32[72,128]{1,0:T(8,128)S(1)}, f32[72,128]{1,0:T(8,128)}, u32[]{:S(2)}) copy-start(f32[72,128]{1,0:T(8,128)} %copy-done.17) | copy-start | bytes 110596
  331.9 5.9 %copy-start.27 = (f32[8,128]{1,0:T(8,128)S(1)}, f32[8,128]{1,0:T(8,128)}, u32[]{:S(2)}) copy-start(f32[8,128]{1,0:T(8,128)} %copy-done.26) | copy-start | bytes 12292
  (11 other events, 7.3 us)

commit v3 on v2

--- a/solution.py
+++ b/solution.py
@@ -597,6 +597,18 @@
             second(job, step).wait_send()
 
 
+def hand_over(*refs):
+    count = len(refs) // 2
+    semaphores = refs[-1]
+    copies = [
+        pltpu.make_async_copy(refs[k], refs[count + k], semaphores.at[k]) for k in range(count)
+    ]
+    for copy in copies:
+        copy.start()
+    for copy in copies:
+        copy.wait()
+
+
 def scatter_sums(terms):
     bfloat = jnp.bfloat16
     shapes = [(term.shape[0] // 16, term.shape[1]) for term in terms]
@@ -608,19 +620,27 @@
     scratch += [pltpu.VMEM((3, *block), bfloat) for block in blocks]
     scratch += [pltpu.SemaphoreType.DMA((len(jobs),))]
     scratch += [pltpu.SemaphoreType.DMA((len(jobs), 3)) for _ in range(4)]
-    return pl.pallas_call(
+    sums = pl.pallas_call(
         functools.partial(scatter_kernel, jobs),
         out_shape=[jax.ShapeDtypeStruct(shape, jnp.float32) for shape in shapes],
         in_specs=[pl.BlockSpec(memory_space=pl.ANY)] * len(terms),
         out_specs=[pl.BlockSpec(memory_space=pltpu.VMEM)] * len(terms),
         scratch_shapes=scratch,
         compiler_params=pltpu.CompilerParams(
-            collective_id=1, has_side_effects=True, vmem_limit_bytes=40000000
+            collective_id=1, has_side_effects=True, vmem_limit_bytes=67043328
         ),
         cost_estimate=pl.CostEstimate(
             flops=2_000_000_000, bytes_accessed=30_000_000, transcendentals=0
         ),
     )(*[term.reshape(4, 4, *shape) for term, shape in zip(terms, shapes)])
+    return pl.pallas_call(
+        hand_over,
+        out_shape=[jax.ShapeDtypeStruct(shape, jnp.float32) for shape in shapes],
+        in_specs=[pl.BlockSpec(memory_space=pltpu.VMEM)] * len(sums),
+        out_specs=[pl.BlockSpec(memory_space=pl.ANY)] * len(sums),
+        scratch_shapes=[pltpu.SemaphoreType.DMA((len(sums),))],
+        compiler_params=pltpu.CompilerParams(vmem_limit_bytes=67043328),
+    )(*sums)
 
 
 def by_parity(field):

time: 340 us -> 331 us (0.974)
  local copies, waits for them, and re-layouts: 49.7 us -> 29.3 us
  Pallas kernels: 207 us -> 219 us
    unnamed x94 -> x28, local copies, waits for them, and re-layouts: 21.8 us -> 1.31 us
    pallas_call x1, Pallas kernels: 111 us -> 121 us  [scatter_sums(): pl.pallas_call(functools.partial(scatter_kernel, jobs), out_shape=[jax.Sh...]
  transfers between devices with their start and end apart: 2 -> 2, of which waited for: 1 -> 1; matrix products, arithmetic and copies ran while one was open for 6% -> 6% of each run, Pallas kernels for 33% -> 37%
where the time goes in v3:
time: 331 us; the launch traced here: 330 us
  Pallas kernels  219 us (66%)
  waiting for transfers between devices  34.1 us (10%)
  local copies, waits for them, and re-layouts  29.3 us (9%)
  matrix products  20.8 us (6%)
  starting transfers between devices  19.2 us (6%)
  other arithmetic  6.52 us (2%)
    pallas_call x1, Pallas kernels, scatter_sums(): pl.pallas_call(functools.partial(scatter_kernel, jobs), out_shape=[jax.Sh...  121 us
    pallas_call x1, Pallas kernels, unet(): pl.pallas_call(unet_kernel, out_shape=[jax.ShapeDtypeStruct(*leaf) for le...  96 us
    all_to_all x1, waiting for transfers between devices, body(): lax.all_to_all(outgoing, 'slab', split_axis=0, concat_axis=0, tiled=True)  34.1 us
    all_to_all x1, starting transfers between devices, body(): lax.all_to_all(slot_grad.reshape(devices, CAP, -1), 'slab', split_axis=0,...  11.2 us
    reshape x5, local copies, waits for them, and re-layouts, flipped(): weight.reshape(9, inward, -1)[::-1].transpose(0, 2, 1).reshape(-1, inward)  8.55 us
    rev x5, local copies, waits for them, and re-layouts, flipped(): weight.reshape(9, inward, -1)[::-1].transpose(0, 2, 1).reshape(-1, inward)  8.53 us
    all_to_all x1, starting transfers between devices, body(): lax.all_to_all(outgoing, 'slab', split_axis=0, concat_axis=0, tiled=True)  8.08 us
  transfers between devices with their start and end apart: 2, of which 1 were waited for; matrix products, arithmetic and copies ran while one was open for 6% of the time, Pallas kernels for 37%

profile of v3, /device:TPU:46, one launch (start us, length us, event | category | flops | bytes accessed | tf_op | source)
XLA Modules:
  0.0 329.8 jit_solution(12640869582653014367)
XLA Ops:
  0.6 0.5 broadcast.103
  1.2 1.3 broadcast_multiply_fusion
  2.7 1.4 select_reduce_fusion
  4.3 0.8 fusion.29
  5.2 3.9 %fusion.10 = bf16[64,128,128]{2,1,0:T(8,128)(2,1)S(1)} fusion(bf16[64,128,128]{2,1,0:T(8,128)(2,1)} %param.16, s32[64,128]{1,0:T(8,128)S(1)} %fusion.29), kind=kOutput, calls=%fused_computation.15 | convolution fusion | flops 270532608 | bytes 4227072 | tf_op jit(solution)/shard_map/bpt,bpc->btc/dot_general | solution.py:704
  9.1 3.6 %fusion = bf16[16,8,16384]{2,1,0:T(8,128)(2,1)} fusion(bf16[8,8,128,128]{3,2,1,0:T(8,128)(2,1)S(1)} %bitcast.87, s32[64]{0:T(128)S(1)} %dynamic_slice.7), kind=kOutput, calls=%fused_computation.2 | convolution fusion | flops 270540800 | bytes 6291712 | tf_op jit(solution)/shard_map/dot_general | solution.py:709
  12.7 8.1 %all-to-all-start = ((bf16[16,8,16384]{2,1,0:T(8,128)(2,1)}), bf16[16,8,16384]{2,1,0:T(8,128)(2,1)}, u32[]{:S(2)}, u32[]{:S(2)}) async-start(bf16[16,8,16384]{2,1,0:T(8,128)(2,1)} %fusion), calls=%async_computation | async-start | bytes 8388608 | tf_op jit(solution)/shard_map/all_to_all | solution.py:713
  21.1 0.7 rev.19
  22.0 0.7 rev.15
  22.8 1.3 copy.73
  24.0 0.7 copy.77
  24.8 1.1 rev.18
  25.9 0.7 copy.75
  26.6 1.1 rev.16
  28.0 6.7 %copy.76 = bf16[9,512,512]{1,2,0:T(8,128)(2,1)} copy(bf16[9,512,512]{2,1,0:T(8,128)(2,1)} %bitcast.89) | data formatting | bytes 9437184 | tf_op jit(solution)/shard_map/reshape | solution.py:24
  34.7 4.8 %rev.17 = bf16[9,512,512]{1,2,0:T(8,128)(2,1)} reverse(bf16[9,512,512]{1,2,0:T(8,128)(2,1)} %copy.76), dimensions={0} | reverse | bytes 9437184 | tf_op jit(solution)/shard_map/rev | solution.py:24
  39.9 34.1 %all-to-all-done = bf16[16,8,16384]{2,1,0:T(8,128)(2,1)} async-done(((bf16[16,8,16384]{2,1,0:T(8,128)(2,1)}), bf16[16,8,16384]{2,1,0:T(8,128)(2,1)}, u32[]{:S(2)}, u32[]{:S(2)}) %all-to-all-start) | async-done | bytes 4194336 | tf_op jit(solution)/shard_map/all_to_all | solution.py:713
  74.1 6.4 %copy.70 = bf16[128,16384]{0,1:T(8,128)(2,1)} copy(bf16[128,16384]{1,0:T(8,128)(2,1)} %bitcast.7) | data formatting | bytes 8388608 | tf_op jit(solution)/shard_map/reshape | solution.py:713
  80.5 3.7 %convolution_bitcast_fusion = f32[16,4,2,32,128]{4,0,3,1,2:T(8,128)S(1)} fusion(bf16[4,32,128,128,1]{3,2,1,0,4:T(8,128)(2,1)} %bitcast.86, bf16[16,2,128,1,1]{2,1,0,4,3:T(2,128)(2,1)S(1)} %bitcast.114), kind=kOutput, calls=%fused_computation.18 | convolution fusion | flops 134217728 | bytes 6299648 | tf_op jit(solution)/shard_map/dot_general | solution.py:716
  84.2 0.7 copy.72
  84.9 1.3 fusion.7.refs_0_
  86.2 96.0 %shard_map.247 = (bf16[16,256,128]{2,1,0:T(8,128)(2,1)}, f32[16,8,128]{2,1,0:T(8,128)}, bf16[1152,128]{1,0:T(8,128)(2,1)}, bf16[512,256]{1,0:T(8,128)(2,1)}, bf1...) custom-call(bf16[16,256,128]{2,1,0:T(8,128)(2,1)} %fusion.7.refs_0_,, ...), custom_call_target="tpu_custom_call" | custom-call | flops 24000000000 | bytes 40000000 | tf_op jit(solution)/shard_map/pallas_call | solution.py:480
  182.3 1.4 copy.93
  184.2 3.2 fusion.1
  187.4 11.2 %all-to-all-start.1 = ((bf16[16,8,16384]{2,1,0:T(8,128)(2,1)}), bf16[16,8,16384]{2,1,0:T(8,128)(2,1)}, u32[]{:S(2)}, u32[]{:S(2)}) async-start(bf16[16,8,16384]{2,1,0:T(8,128)(2,1)} %fusion.1), calls=%async_computation.1 | async-start | bytes 8388608 | tf_op jit(solution)/shard_map/all_to_all | solution.py:746
  198.6 120.5 %shard_map.248 = (f32[72,128]{1,0:T(8,128)}, f32[32,256]{1,0:T(8,128)}, f32[144,256]{1,0:T(8,128)}, f32[64,512]{1,0:T(8,128)}, f32[288,512]{1,0:T(8,128)}, /*ind...) custom-call(bf16[4,4,72,128]{3,2,1,0:T(8,128)(2,1)} %bitcast.105, ...), custom_call_target="tpu_custom_call" | custom-call | flops 2000000000 | bytes 30000000 | tf_op jit(solution)/shard_map/pallas_call | solution.py:623
  319.1 2.4 shard_map.249
  321.5 1.0 slice_reduce_fusion
  322.6 0.5 broadcast_multiply_fusion.1
  323.1 2.9 fusion.12
  326.1 0.6 copy.85
  326.8 3.0 fusion.11
  (39 shorter events, 2.2 us)
Async XLA Ops:
  4.3 4.7 %copy-start.11 = (s32[64]{0:T(128)}, s32[64]{0:T(128)S(1)}, u32[]{:S(2)}) copy-start(s32[64]{0:T(128)S(1)} %dynamic_slice.7) | copy-start | bytes 772
  5.2 3.9 %copy-start.4 = (s32[64,128]{1,0:T(8,128)}, s32[64,128]{1,0:T(8,128)S(1)}, u32[]{:S(2)}) copy-start(s32[64,128]{1,0:T(8,128)S(1)} %fusion.29) | copy-start | bytes 98308
  12.7 8.1 %copy-start.7 = (bf16[1152,128]{1,0:T(8,128)(2,1)S(1)}, bf16[1152,128]{1,0:T(8,128)(2,1)}, u32[]{:S(2)}) copy-start(bf16[1152,128]{1,0:T(8,128)(2,1)} %refs_10_.1) | copy-start | bytes 884740
  12.7 9.1 %copy-start.6 = (bf16[1152,128]{1,0:T(8,128)(2,1)S(1)}, bf16[1152,128]{1,0:T(8,128)(2,1)}, u32[]{:S(2)}) copy-start(bf16[1152,128]{1,0:T(8,128)(2,1)} %refs_2_.1) | copy-start | bytes 884740
  12.7 61.3 %all-to-all-start = ((bf16[16,8,16384]{2,1,0:T(8,128)(2,1)}), bf16[16,8,16384]{2,1,0:T(8,128)(2,1)}, u32[]{:S(2)}, u32[]{:S(2)}) async-start(bf16[16,8,16384]{2,1,0:T(8,128)(2,1)} %fusion), calls=%async_computation | async-start | bytes 8388608 | tf_op jit(solution)/shard_map/all_to_all | solution.py:713
  20.8 2.0 copy-start.3
  20.8 3.2 copy-start.1
  24.0 1.9 copy-start
  25.9 1.8 copy-start.2
  34.7 4.8 %copy-start.10 = (s32[1024,1]{0,1:T(1,128)S(1)}, s32[1024,1]{0,1:T(1,128)}, u32[]{:S(2)}) copy-start(s32[1024,1]{0,1:T(1,128)} %param.18) | copy-start | bytes 12292
  34.7 4.9 %copy-start.12 = (s32[1024]{0:T(1024)S(1)}, s32[1024]{0:T(1024)}, u32[]{:S(2)}) copy-start(s32[1024]{0:T(1024)} %param.19) | copy-start | bytes 12292
  39.9 40.6 %copy-start.8 = (bf16[32,128]{1,0:T(8,128)(2,1)}, bf16[32,128]{1,0:T(8,128)(2,1)S(1)}, u32[]{:S(2)}) copy-start(bf16[32,128]{1,0:T(8,128)(2,1)S(1)} %convolution_convert_fusion.3) | copy-start | bytes 24580
  182.3 1.9 copy-start.9
  187.4 135.7 %all-to-all-start.1 = ((bf16[16,8,16384]{2,1,0:T(8,128)(2,1)}), bf16[16,8,16384]{2,1,0:T(8,128)(2,1)}, u32[]{:S(2)}, u32[]{:S(2)}) async-start(bf16[16,8,16384]{2,1,0:T(8,128)(2,1)} %fusion.1), calls=%async_computation.1 | async-start | bytes 8388608 | tf_op jit(solution)/shard_map/all_to_all | solution.py:746
  326.1 0.8 copy-start.5

commit v4 on v3

--- a/solution.py
+++ b/solution.py
@@ -643,6 +643,95 @@
     )(*sums)
 
 
+def repeat(bound, body, unroll):
+    def step(index, carry):
+        body(index)
+        return carry
+
+    lax.fori_loop(0, bound, step, 0, unroll=unroll)
+
+
+def cell_mask(cells, block):
+    row = cells[pl.ds(block, 1), :]
+    place = lax.broadcasted_iota(jnp.int32, (TILE, row.shape[1]), 0)
+    return (jnp.broadcast_to(row, place.shape) == place).astype(jnp.bfloat16)
+
+
+def deposit_kernel(slots, cells, features, out):
+    zero = jnp.zeros((TILE, TILE), jnp.bfloat16)
+
+    def clear(slot):
+        out[slot] = zero
+
+    repeat(out.shape[0], clear, 8)
+
+    def deposit(block):
+        value = jnp.dot(
+            cell_mask(cells, block), features[block], preferred_element_type=jnp.float32
+        )
+        out[slots[block]] = value.astype(jnp.bfloat16)
+
+    repeat(features.shape[0], deposit, 8)
+
+
+def splat_kernel(tiles, incoming, base, out, canvas):
+    zero = jnp.zeros((TILE, TILE), jnp.float32)
+
+    def clear(tile):
+        canvas[tile] = zero
+
+    repeat(canvas.shape[0], clear, 3)
+
+    def add(slot):
+        tile = tiles[slot]
+        canvas[tile] = canvas[tile] + incoming[slot].astype(jnp.float32)
+
+    repeat(incoming.shape[0], add, 4)
+
+    def finish(row):
+        for k in range(4):
+            for half in range(2):
+                cells = slice(k * 64 + half * 32, k * 64 + half * 32 + 32)
+                total = base[row, cells].astype(jnp.float32)
+                total = total + canvas[2 * row + half, k * 32 : k * 32 + 32]
+                out[row, cells] = total.astype(jnp.bfloat16)
+
+    repeat(out.shape[0], finish, 2)
+
+
+def pick_kernel(tiles, gradient, out):
+    def pick(slot):
+        tile = tiles[slot]
+        row, half = lax.div(tile, 2), lax.rem(tile, 2)
+        for k in range(4):
+            cells = pl.ds(pl.multiple_of(k * 64 + half * 32, 32), 32)
+            out[slot, k * 32 : k * 32 + 32] = gradient[row, cells]
+
+    repeat(out.shape[0], pick, 4)
+
+
+def camera_kernel(slots, cells, returned, out):
+    def camera(block):
+        out[block] = outer(cell_mask(cells, block), returned[slots[block]]).astype(jnp.bfloat16)
+
+    repeat(out.shape[0], camera, 8)
+
+
+def local_call(kernel, shape, operands, scratch=()):
+    vector = pl.BlockSpec(memory_space=pltpu.VMEM)
+    return pl.pallas_call(
+        kernel,
+        out_shape=jax.ShapeDtypeStruct(shape, jnp.bfloat16),
+        in_specs=[pl.BlockSpec(memory_space=pltpu.SMEM)] + [vector] * (len(operands) - 1),
+        out_specs=vector,
+        scratch_shapes=scratch,
+        compiler_params=pltpu.CompilerParams(vmem_limit_bytes=40000000),
+        cost_estimate=pl.CostEstimate(
+            flops=400_000_000, bytes_accessed=8_000_000, transcendentals=0
+        ),
+    )(*operands)
+
+
 def by_parity(field):
     rows, across, channels = field.shape
     return (
@@ -687,37 +776,30 @@
     slot_number = owners * CAP + ranking
     local_slot = lax.dynamic_slice_in_dim(slot_number, device * BLK_DEV, BLK_DEV)
     slot_range = jnp.arange(slot_count, dtype=jnp.int32)
-    send_map = (local_slot[None, :] == slot_range[:, None]).astype(bfloat)
     arrival = sources * CAP + ranking
     receive_map = ((arrival[None, :] == slot_range[:, None]) & (owners[None, :] == device)).astype(
         jnp.int32
     )
-    tile_onehot = (owner_tile[:, None] == jnp.arange(tile_count, dtype=jnp.int32)[None, :]).astype(
-        jnp.int32
-    )
-    placement = jnp.einsum("bt,sb->ts", tile_onehot, receive_map).astype(bfloat)
-    cell_range = jnp.arange(TILE, dtype=jnp.int32)
+    received = jnp.sum(receive_map, axis=1)
+    slot_tiles = jnp.sum(receive_map * owner_tile[None, :], axis=1)
+    landing_tiles = jnp.where(received > 0, slot_tiles, tile_count)
     local_cells = lax.dynamic_slice_in_dim(cell_index, device * BLK_DEV, BLK_DEV)
     local_cells = local_cells % 2 * 64 + local_cells // 2 % 2 * 32 + local_cells // 4
-    cell_onehot = (local_cells[:, :, None] == cell_range[None, None, :]).astype(bfloat)
-    payload = (
-        jnp.einsum("bpt,bpc->btc", cell_onehot, camera_features, preferred_element_type=single)
-        .astype(bfloat)
-        .reshape(BLK_DEV, -1)
-    )
-    outgoing = (
-        jnp.dot(send_map, payload, preferred_element_type=single)
-        .astype(bfloat)
-        .reshape(devices, CAP, -1)
-    )
-    incoming = lax.all_to_all(outgoing, "slab", split_axis=0, concat_axis=0, tiled=True).reshape(
-        slot_count, -1
-    )
-    canvas = jnp.dot(placement, incoming, preferred_element_type=single)
-    canvas = canvas.reshape(height, 2, 4, 32, channels).transpose(0, 2, 1, 3, 4)
-    level_zero = (
-        by_parity(base_map).astype(single) + canvas.reshape(height, across, channels)
-    ).astype(bfloat)
+    wire = (devices, CAP * TILE, channels)
+    outgoing = local_call(
+        deposit_kernel,
+        (slot_count, TILE, channels),
+        (local_slot, local_cells, camera_features),
+    )
+    incoming = lax.all_to_all(
+        outgoing.reshape(wire), "slab", split_axis=0, concat_axis=0, tiled=True
+    ).reshape(slot_count, TILE, channels)
+    level_zero = local_call(
+        splat_kernel,
+        (height, across, channels),
+        (landing_tiles, incoming, by_parity(base_map)),
+        [pltpu.VMEM((tile_count + 1, TILE, channels), single)],
+    )
     level_zero_grad, losses, *terms = unet(
         level_zero,
         by_parity(targets),
@@ -738,23 +820,15 @@
         flipped(fine_merge),
     )
     row_loss = jnp.sum(losses[:, 0, :], axis=1) / (across * K)
-    level_zero_grad = level_zero_grad.reshape(height, 4, 2, 32, channels).transpose(0, 2, 1, 3, 4)
-    tiles_grad = level_zero_grad.reshape(tile_count, -1)
-    slot_grad = jnp.einsum(
-        "ts,tl->sl", placement, tiles_grad, preferred_element_type=single
-    ).astype(bfloat)
+    slot_grad = local_call(
+        pick_kernel, (slot_count, TILE, channels), (slot_tiles, level_zero_grad)
+    )
     returned = lax.all_to_all(
-        slot_grad.reshape(devices, CAP, -1), "slab", split_axis=0, concat_axis=0, tiled=True
-    ).reshape(slot_count, -1)
-    own_blocks = jnp.einsum("sb,sl->bl", send_map, returned, preferred_element_type=single).astype(
-        bfloat
-    )
-    camera_grad = jnp.einsum(
-        "bpt,btc->bpc",
-        cell_onehot,
-        own_blocks.reshape(BLK_DEV, TILE, channels),
-        preferred_element_type=single,
-    ).astype(bfloat)
+        slot_grad.reshape(wire), "slab", split_axis=0, concat_axis=0, tiled=True
+    ).reshape(slot_count, TILE, channels)
+    camera_grad = local_call(
+        camera_kernel, camera_features.shape, (local_slot, local_cells, returned)
+    )
     sums = scatter_sums(terms)
     return (camera_grad, row_loss, *sums)
 

time: 331 us -> 323 us (0.976)
  matrix products: 20.8 us -> 0 us
  Pallas kernels: 219 us -> 233 us
    dot_general x6 -> x0, matrix products: 20.4 us -> none  [the longest x1 3.89 us: body(): jnp.einsum('bpt,bpc->btc', cell_onehot, camera_features, preferred_elemen...]
    pallas_call x0 -> x4, Pallas kernels: none -> 13.9 us  [local_call(): pl.pallas_call(kernel, out_shape=jax.ShapeDtypeStruct(shape, jnp.bfloat16...]
    unnamed x28 -> x37, local copies, waits for them, and re-layouts: 1.31 us -> 10.9 us
    reshape x3 -> x0, local copies, waits for them, and re-layouts: 8.3 us -> none  [the longest x1 6.44 us: body(): lax.all_to_all(outgoing, 'slab', split_axis=0, concat_axis=0, tiled=True)]
  transfers between devices with their start and end apart: 2 -> 2, of which waited for: 1 -> 1; matrix products, arithmetic and copies ran while one was open for 6% -> 7% of each run, Pallas kernels for 37% -> 38%
where the time goes in v4:
time: 323 us; the launch traced here: 322 us
  Pallas kernels  233 us (72%)
  waiting for transfers between devices  32.9 us (10%)
  local copies, waits for them, and re-layouts  30.8 us (10%)
  starting transfers between devices  19.3 us (6%)
  other arithmetic  5.41 us (2%)
    pallas_call x1, Pallas kernels, scatter_sums(): pl.pallas_call(functools.partial(scatter_kernel, jobs), out_shape=[jax.Sh...  121 us
    pallas_call x1, Pallas kernels, unet(): pl.pallas_call(unet_kernel, out_shape=[jax.ShapeDtypeStruct(*leaf) for le...  96 us
    all_to_all x1, waiting for transfers between devices, body(): lax.all_to_all(outgoing.reshape(wire), 'slab', split_axis=0, concat_axis=...  32.9 us
    pallas_call x4, Pallas kernels, local_call(): pl.pallas_call(kernel, out_shape=jax.ShapeDtypeStruct(shape, jnp.bfloat16...  13.9 us
    all_to_all x1, starting transfers between devices, body(): lax.all_to_all(slot_grad.reshape(wire), 'slab', split_axis=0, concat_axis...  11.2 us
    unnamed x37, local copies, waits for them, and re-layouts  10.9 us
    reshape x5, local copies, waits for them, and re-layouts, flipped(): weight.reshape(9, inward, -1)[::-1].transpose(0, 2, 1).reshape(-1, inward)  9.49 us
    rev x5, local copies, waits for them, and re-layouts, flipped(): weight.reshape(9, inward, -1)[::-1].transpose(0, 2, 1).reshape(-1, inward)  8.53 us
  transfers between devices with their start and end apart: 2, of which 1 were waited for; matrix products, arithmetic and copies ran while one was open for 7% of the time, Pallas kernels for 38%

profile of v4, /device:TPU:46, one launch (start us, length us, event | category | flops | bytes accessed | tf_op | source)
XLA Modules:
  0.0 322.4 jit_solution(2605395398663473507)
XLA Ops:
  1.2 1.3 fusion.21
  2.7 1.4 select_reduce_fusion.1
  4.3 0.8 fusion.8.cells
  5.2 1.6 copy-done.2
  6.8 2.9 shard_map.247
  9.7 2.0 copy-done.1
  11.7 8.1 %all-to-all-start = ((bf16[16,1024,128]{2,1,0:T(8,128)(2,1)}), bf16[16,1024,128]{2,1,0:T(8,128)(2,1)}, u32[]{:S(2)}, u32[]{:S(2)}) async-start(bf16[16,1024,128]{2,1,0:T(8,128)(2,1)} %bitcast.45), calls=%async_computation | async-start | bytes 8388608 | tf_op jit(solution)/shard_map/all_to_all | solution.py:794
  20.1 0.7 rev.19
  21.0 0.7 rev.15
  22.1 1.3 copy.56
  23.3 1.7 copy.60
  25.0 1.1 rev.18
  26.1 0.7 copy.58
  26.8 1.1 rev.16
  27.9 6.7 %copy.59 = bf16[9,512,512]{1,2,0:T(8,128)(2,1)} copy(bf16[9,512,512]{2,1,0:T(8,128)(2,1)} %bitcast.47) | data formatting | bytes 9437184 | tf_op jit(solution)/shard_map/reshape | solution.py:24
  34.6 4.8 %rev.17 = bf16[9,512,512]{1,2,0:T(8,128)(2,1)} reverse(bf16[9,512,512]{1,2,0:T(8,128)(2,1)} %copy.59), dimensions={0} | reverse | bytes 9437184 | tf_op jit(solution)/shard_map/rev | solution.py:24
  40.2 32.9 %all-to-all-done = bf16[16,1024,128]{2,1,0:T(8,128)(2,1)} async-done(((bf16[16,1024,128]{2,1,0:T(8,128)(2,1)}), bf16[16,1024,128]{2,1,0:T(8,128)(2,1)}, u32[]{:S(2)}, u32[]{:S(2)}) %all-to-all-start) | async-done | bytes 4194336 | tf_op jit(solution)/shard_map/all_to_all | solution.py:794
  73.1 3.6 %shard_map.248.refs_0_ = bf16[16,256,128]{2,1,0:T(8,128)(2,1)S(1)} custom-call(s32[128]{0:T(128)S(1)} %compare_select_fusion.tiles, bf16[128,128,128]{2,1,0:T(8,128)(2,1)} %bitcast.2.incoming, bf16[16,256,128]{2,1,0:T(8,128)(2,1)S(1)} %bitcast.46), custom_call_target="tpu_custom_call" | custom-call | flops 400000000 | bytes 8000000 | tf_op jit(solution)/shard_map/pallas_call | solution.py:722
  76.7 1.0 copy-done.3
  77.7 96.0 %shard_map.249 = (bf16[16,256,128]{2,1,0:T(8,128)(2,1)}, f32[16,8,128]{2,1,0:T(8,128)}, bf16[1152,128]{1,0:T(8,128)(2,1)}, bf16[512,256]{1,0:T(8,128)(2,1)}, bf1...) custom-call(bf16[16,256,128]{2,1,0:T(8,128)(2,1)} %copy-done.3, ...), custom_call_target="tpu_custom_call" | custom-call | flops 24000000000 | bytes 40000000 | tf_op jit(solution)/shard_map/pallas_call | solution.py:480
  173.7 1.2 copy-done.4
  174.9 0.7 copy-done.10
  175.6 1.8 shard_map.250
  177.3 2.0 copy-done
  179.3 11.2 %all-to-all-start.1 = ((bf16[16,1024,128]{2,1,0:T(8,128)(2,1)}), bf16[16,1024,128]{2,1,0:T(8,128)(2,1)}, u32[]{:S(2)}, u32[]{:S(2)}) async-start(bf16[16,1024,128]{2,1,0:T(8,128)(2,1)} %bitcast.44), calls=%async_computation.1 | async-start | bytes 8388608 | tf_op jit(solution)/shard_map/all_to_all | solution.py:826
  190.5 120.9 %shard_map.252 = (f32[72,128]{1,0:T(8,128)}, f32[32,256]{1,0:T(8,128)}, f32[144,256]{1,0:T(8,128)}, f32[64,512]{1,0:T(8,128)}, f32[288,512]{1,0:T(8,128)}, /*ind...) custom-call(bf16[4,4,72,128]{3,2,1,0:T(8,128)(2,1)} %bitcast.61, ...), custom_call_target="tpu_custom_call" | custom-call | flops 2000000000 | bytes 30000000 | tf_op jit(solution)/shard_map/pallas_call | solution.py:623
  311.4 2.4 shard_map.253
  313.8 1.0 slice_reduce_fusion
  314.9 0.5 broadcast_multiply_fusion.1
  315.4 0.8 copy-done.6
  316.2 0.6 copy-done.8
  316.8 5.6 %shard_map.251 = bf16[64,128,128]{2,1,0:T(8,128)(2,1)} custom-call(s32[64]{0:T(128)S(1)} %copy-done.8, s32[64,128]{1,0:T(8,128)S(1)} %copy-done.6, bf16[128,128,128]{2,1,0:T(8,128)(2,1)} %bitcast.25.returned), custom_call_target="tpu_custom_call" | custom-call | flops 400000000 | bytes 8000000 | tf_op jit(solution)/shard_map/pallas_call | solution.py:722
  (42 shorter events, 2.4 us)
Async XLA Ops:
  4.3 5.3 %copy-start.7 = (s32[64]{0:T(128)}, s32[64]{0:T(128)S(1)}, u32[]{:S(2)}) copy-start(s32[64]{0:T(128)S(1)} %dynamic_slice.6.slots) | copy-start | bytes 772
  5.2 1.6 copy-start.2
  6.8 2.9 copy-start.5
  9.7 2.0 copy-start.1
  11.7 8.1 %copy-start.15 = (bf16[1152,128]{1,0:T(8,128)(2,1)S(1)}, bf16[1152,128]{1,0:T(8,128)(2,1)}, u32[]{:S(2)}) copy-start(bf16[1152,128]{1,0:T(8,128)(2,1)} %refs_10_.1) | copy-start | bytes 884740
  11.7 9.1 %copy-start.14 = (bf16[1152,128]{1,0:T(8,128)(2,1)S(1)}, bf16[1152,128]{1,0:T(8,128)(2,1)}, u32[]{:S(2)}) copy-start(bf16[1152,128]{1,0:T(8,128)(2,1)} %refs_2_.1) | copy-start | bytes 884740
  11.7 61.4 %all-to-all-start = ((bf16[16,1024,128]{2,1,0:T(8,128)(2,1)}), bf16[16,1024,128]{2,1,0:T(8,128)(2,1)}, u32[]{:S(2)}, u32[]{:S(2)}) async-start(bf16[16,1024,128]{2,1,0:T(8,128)(2,1)} %bitcast.45), calls=%async_computation | async-start | bytes 8388608 | tf_op jit(solution)/shard_map/all_to_all | solution.py:794
  19.8 2.0 copy-start.12
  19.8 2.2 copy-start.13
  23.3 2.8 copy-start.11
  34.6 4.8 %copy-start.16 = (s32[1024,1]{0,1:T(1,128)S(1)}, s32[1024,1]{0,1:T(1,128)}, u32[]{:S(2)}) copy-start(s32[1024,1]{0,1:T(1,128)} %param.18) | copy-start | bytes 12292
  34.6 4.9 %copy-start.17 = (s32[1024]{0:T(1024)S(1)}, s32[1024]{0:T(1024)}, u32[]{:S(2)}) copy-start(s32[1024]{0:T(1024)} %param.19) | copy-start | bytes 12292
  39.7 0.5 copy-start.9
  76.7 1.0 copy-start.3
  173.7 1.2 copy-start.4
  174.9 0.7 copy-start.10
  177.3 2.0 copy-start
  179.3 136.1 %all-to-all-start.1 = ((bf16[16,1024,128]{2,1,0:T(8,128)(2,1)}), bf16[16,1024,128]{2,1,0:T(8,128)(2,1)}, u32[]{:S(2)}, u32[]{:S(2)}) async-start(bf16[16,1024,128]{2,1,0:T(8,128)(2,1)} %bitcast.44), calls=%async_computation.1 | async-start | bytes 8388608 | tf_op jit(solution)/shard_map/all_to_all | solution.py:826
  315.4 0.8 copy-start.6
  316.2 0.6 copy-start.8

commit v5 on v4

--- a/solution.py
+++ b/solution.py
@@ -94,6 +94,12 @@
 
 
 def unet_kernel(*refs):
+    loads = [
+        pltpu.make_async_copy(refs[2 + k], refs[k - 16], refs[-1].at[k]) for k in range(15)
+    ]
+    refs = refs[:2] + refs[-16:-1] + refs[17:-16]
+    for k in (0, 1, 2, 3, 4, 5, 6, 7, 8, 9, 14, 13, 12, 11, 10):
+        loads[k].start()
     (
         zero_ref, labels_ref, fine_conv, fine_down, middle_conv, middle_down, coarse_conv,
         coarse_up, middle_merge, middle_up, fine_merge, head, flip_fine, flip_middle,
@@ -197,6 +203,7 @@
             pre_fine[rows, k * 128 : (k + 1) * 128] = part
             hid_fine[rows, k * 128 : (k + 1) * 128] = jax.nn.silu(part).astype(bfloat)
 
+    loads[0].wait()
     fine_rows(fine_step, True, False)
     take_edges(field_zero, 16)
     fine_rows(fine_step, False, True)
@@ -210,6 +217,7 @@
         edges_middle[slot, 0] = field[pl.ds(128, 128), 256:512]
         edges_middle[slot, 1] = field[pl.ds(8 * 128, 128), 256:512]
 
+    loads[1].wait()
     middle_rows(one_step, False, True)
     middle_edges(field_one, 0)
     send_edges(edges_middle.at[0, 0], edges_middle.at[0, 1], halo_middle, 1, 0)
@@ -223,6 +231,7 @@
             pre_middle[rows, k * 256 : (k + 1) * 256] = part
             hid_middle[rows, k * 256 : (k + 1) * 256] = jax.nn.silu(part).astype(bfloat)
 
+    loads[2].wait()
     middle_rows(middle_step, True, False)
     take_edges(field_one, 8)
     middle_rows(middle_step, False, True)
@@ -239,8 +248,10 @@
             field[window(step * 64, 256), :], weight[window(step * 1536, 1536), :]
         )
 
+    loads[3].wait()
     value = times(hid_middle[...], middle_down[...]).astype(bfloat)
     spread_coarse(field_two, value, 0, 2)
+    loads[4].wait()
     pre_coarse[...] = coarse_part(field_two, coarse_conv, 1)
     take_edges(field_two, 4)
 
@@ -260,6 +271,7 @@
             )
             put_row(field_merge, 2 * at + i + 1, row)
 
+    loads[5].wait()
     middle_rows(join_middle, False, True)
     middle_edges(field_merge, 1)
     send_edges(edges_middle.at[1, 0], edges_middle.at[1, 1], halo_middle, 3, 1)
@@ -271,6 +283,7 @@
         pre_merge[rows, :] = pre
         out_middle[rows, :] = jax.nn.silu(pre).astype(bfloat)
 
+    loads[6].wait()
     middle_rows(merge_step, True, False)
     take_edges(field_merge, 8)
     middle_rows(merge_step, False, True)
@@ -289,6 +302,7 @@
         edges_fine[slot, 0] = field[pl.ds(256, 256), 128:256]
         edges_fine[slot, 1] = field[pl.ds(16 * 256, 256), 128:256]
 
+    loads[7].wait()
     fine_rows(join_fine, False, True)
     fine_edges(field_top, 0)
     send_edges(edges_fine.at[0, 0], edges_fine.at[0, 1], halo_fine, 4, 1)
@@ -313,6 +327,8 @@
             down = backward(slope, head[...]) * (level * (1.0 + pre[one] * (1.0 - level)))
             put_row(field_fine, 2 * at + i + 1, down.astype(bfloat))
 
+    loads[8].wait()
+    loads[9].wait()
     fine_rows(top_step, True, False)
     take_edges(field_top, 16)
     fine_rows(top_step, False, True)
@@ -341,6 +357,7 @@
         for k in range(4):
             grad_fine[rows, k * 128 : (k + 1) * 128] = value[k * 128 : (k + 1) * 128]
 
+    loads[14].wait()
     each(0, 8, grad_fine_step)
 
     def back_merge_step(at):
@@ -375,6 +392,7 @@
         for k in range(4):
             grad_middle[rows, k * 256 : (k + 1) * 256] = value[k * 64 : (k + 1) * 64]
 
+    loads[13].wait()
     each(0, 4, grad_middle_step)
 
     value = backward(grad_middle[...], coarse_up[...]) * silu_slope(pre_coarse[...])
@@ -388,6 +406,7 @@
 
     each(0, 3, coarse_weight)
     take_edges(field_coarse, 4)
+    loads[12].wait()
     pre_coarse[...] = coarse_part(field_coarse, flip_coarse, 1)
 
     def coarse_back(index):
@@ -419,6 +438,7 @@
         value = times(tap_rows(field_middle, 2 * at, 2, 128), flip_middle[...]).astype(bfloat)
         grad_one[window(at * 256, 256), :] = value
 
+    loads[11].wait()
     each(0, 4, grad_one_step)
 
     def back_fine_step(at):
@@ -443,6 +463,7 @@
         for i in range(2):
             zero_grad[2 * at + i] = value[i * 256 : (i + 1) * 256]
 
+    loads[10].wait()
     each(0, 8, zero_step)
 
     for top, bottom, halo, exchange, slot in started:
@@ -480,10 +501,13 @@
     return pl.pallas_call(
         unet_kernel,
         out_shape=[jax.ShapeDtypeStruct(*leaf) for leaf in shapes],
-        in_specs=[pl.BlockSpec(memory_space=pltpu.VMEM)] * len(operands),
+        in_specs=[pl.BlockSpec(memory_space=pltpu.VMEM)] * 2
+        + [pl.BlockSpec(memory_space=pl.ANY)] * 15,
         out_specs=[pl.BlockSpec(memory_space=pltpu.VMEM)] * len(shapes),
         scratch_shapes=[pltpu.VMEM(*leaf) for leaf in scratch]
-        + [pltpu.SemaphoreType.DMA((10, 2)), pltpu.SemaphoreType.DMA((10, 2))],
+        + [pltpu.SemaphoreType.DMA((10, 2)), pltpu.SemaphoreType.DMA((10, 2))]
+        + [pltpu.VMEM(weight.shape, bfloat) for weight in operands[2:]]
+        + [pltpu.SemaphoreType.DMA((15,))],
         compiler_params=pltpu.CompilerParams(
             collective_id=0, has_side_effects=True, vmem_limit_bytes=67043328
         ),

time: 323 us -> 318 us (0.985)
  Pallas kernels: 233 us -> 228 us
    pallas_call x1, Pallas kernels: 96 us -> 91.3 us  [unet(): pl.pallas_call(unet_kernel, out_shape=[jax.ShapeDtypeStruct(*leaf) for le...]
  transfers between devices with their start and end apart: 2 -> 2, of which waited for: 1 -> 1; matrix products, arithmetic and copies ran while one was open for 7% -> 7% of each run, Pallas kernels for 38% -> 39%
where the time goes in v5:
time: 318 us; the launch traced here: 317 us
  Pallas kernels  228 us (72%)
  waiting for transfers between devices  32.9 us (10%)
  local copies, waits for them, and re-layouts  30.8 us (10%)
  starting transfers between devices  19.2 us (6%)
  other arithmetic  5.41 us (2%)
    pallas_call x1, Pallas kernels, scatter_sums(): pl.pallas_call(functools.partial(scatter_kernel, jobs), out_shape=[jax.Sh...  121 us
    pallas_call x1, Pallas kernels, unet(): pl.pallas_call(unet_kernel, out_shape=[jax.ShapeDtypeStruct(*leaf) for le...  91.3 us
    all_to_all x1, waiting for transfers between devices, body(): lax.all_to_all(outgoing.reshape(wire), 'slab', split_axis=0, concat_axis=...  32.9 us
    pallas_call x4, Pallas kernels, local_call(): pl.pallas_call(kernel, out_shape=jax.ShapeDtypeStruct(shape, jnp.bfloat16...  13.8 us
    all_to_all x1, starting transfers between devices, body(): lax.all_to_all(slot_grad.reshape(wire), 'slab', split_axis=0, concat_axis...  11.1 us
    unnamed x37, local copies, waits for them, and re-layouts  10.9 us
    reshape x5, local copies, waits for them, and re-layouts, flipped(): weight.reshape(9, inward, -1)[::-1].transpose(0, 2, 1).reshape(-1, inward)  9.49 us
    rev x5, local copies, waits for them, and re-layouts, flipped(): weight.reshape(9, inward, -1)[::-1].transpose(0, 2, 1).reshape(-1, inward)  8.53 us
  transfers between devices with their start and end apart: 2, of which 1 were waited for; matrix products, arithmetic and copies ran while one was open for 7% of the time, Pallas kernels for 39%

profile of v5, /device:TPU:46, one launch (start us, length us, event | category | flops | bytes accessed | tf_op | source)
XLA Modules:
  0.0 317.4 jit_solution(17883370698177109036)
XLA Ops:
  1.2 1.3 fusion.21
  2.7 1.4 select_reduce_fusion.1
  4.3 0.8 fusion.8.cells
  5.2 1.6 copy-done.2
  6.8 2.9 shard_map.247
  9.7 2.0 copy-done.1
  11.7 8.1 %all-to-all-start = ((bf16[16,1024,128]{2,1,0:T(8,128)(2,1)}), bf16[16,1024,128]{2,1,0:T(8,128)(2,1)}, u32[]{:S(2)}, u32[]{:S(2)}) async-start(bf16[16,1024,128]{2,1,0:T(8,128)(2,1)} %bitcast.45), calls=%async_computation | async-start | bytes 8388608 | tf_op jit(solution)/shard_map/all_to_all | solution.py:818
  20.1 0.7 rev.19
  21.0 0.7 rev.15
  22.1 1.3 copy.56
  23.3 1.7 copy.60
  25.0 1.1 rev.18
  26.1 0.7 copy.58
  26.8 1.1 rev.16
  27.9 6.7 %copy.59 = bf16[9,512,512]{1,2,0:T(8,128)(2,1)} copy(bf16[9,512,512]{2,1,0:T(8,128)(2,1)} %bitcast.47) | data formatting | bytes 9437184 | tf_op jit(solution)/shard_map/reshape | solution.py:24
  34.6 4.8 %rev.17 = bf16[9,512,512]{1,2,0:T(8,128)(2,1)} reverse(bf16[9,512,512]{1,2,0:T(8,128)(2,1)} %copy.59), dimensions={0} | reverse | bytes 9437184 | tf_op jit(solution)/shard_map/rev | solution.py:24
  40.2 32.9 %all-to-all-done = bf16[16,1024,128]{2,1,0:T(8,128)(2,1)} async-done(((bf16[16,1024,128]{2,1,0:T(8,128)(2,1)}), bf16[16,1024,128]{2,1,0:T(8,128)(2,1)}, u32[]{:S(2)}, u32[]{:S(2)}) %all-to-all-start) | async-done | bytes 4194336 | tf_op jit(solution)/shard_map/all_to_all | solution.py:818
  73.1 3.5 %shard_map.248.refs_0_ = bf16[16,256,128]{2,1,0:T(8,128)(2,1)S(1)} custom-call(s32[128]{0:T(128)S(1)} %compare_select_fusion.tiles, bf16[128,128,128]{2,1,0:T(8,128)(2,1)} %bitcast.2.incoming, bf16[16,256,128]{2,1,0:T(8,128)(2,1)S(1)} %bitcast.46), custom_call_target="tpu_custom_call" | custom-call | flops 400000000 | bytes 8000000 | tf_op jit(solution)/shard_map/pallas_call | solution.py:746
  76.6 1.0 copy-done.3
  77.6 91.3 %shard_map.249 = (bf16[16,256,128]{2,1,0:T(8,128)(2,1)}, f32[16,8,128]{2,1,0:T(8,128)}, bf16[1152,128]{1,0:T(8,128)(2,1)}, bf16[512,256]{1,0:T(8,128)(2,1)}, bf1...) custom-call(bf16[16,256,128]{2,1,0:T(8,128)(2,1)} %copy-done.3, ...), custom_call_target="tpu_custom_call" | custom-call | flops 24000000000 | bytes 40000000 | tf_op jit(solution)/shard_map/pallas_call | solution.py:501
  168.9 1.2 copy-done.4
  170.1 0.7 copy-done.10
  170.8 1.8 shard_map.250
  172.5 2.0 copy-done
  174.5 11.1 %all-to-all-start.1 = ((bf16[16,1024,128]{2,1,0:T(8,128)(2,1)}), bf16[16,1024,128]{2,1,0:T(8,128)(2,1)}, u32[]{:S(2)}, u32[]{:S(2)}) async-start(bf16[16,1024,128]{2,1,0:T(8,128)(2,1)} %bitcast.44), calls=%async_computation.1 | async-start | bytes 8388608 | tf_op jit(solution)/shard_map/all_to_all | solution.py:850
  185.6 120.8 %shard_map.252 = (f32[72,128]{1,0:T(8,128)}, f32[32,256]{1,0:T(8,128)}, f32[144,256]{1,0:T(8,128)}, f32[64,512]{1,0:T(8,128)}, f32[288,512]{1,0:T(8,128)}, /*ind...) custom-call(bf16[4,4,72,128]{3,2,1,0:T(8,128)(2,1)} %bitcast.61, ...), custom_call_target="tpu_custom_call" | custom-call | flops 2000000000 | bytes 30000000 | tf_op jit(solution)/shard_map/pallas_call | solution.py:647
  306.4 2.4 shard_map.253
  308.8 1.0 slice_reduce_fusion
  309.9 0.5 broadcast_multiply_fusion.1
  310.4 0.8 copy-done.6
  311.2 0.6 copy-done.8
  311.7 5.6 %shard_map.251 = bf16[64,128,128]{2,1,0:T(8,128)(2,1)} custom-call(s32[64]{0:T(128)S(1)} %copy-done.8, s32[64,128]{1,0:T(8,128)S(1)} %copy-done.6, bf16[128,128,128]{2,1,0:T(8,128)(2,1)} %bitcast.25.returned), custom_call_target="tpu_custom_call" | custom-call | flops 400000000 | bytes 8000000 | tf_op jit(solution)/shard_map/pallas_call | solution.py:746
  (42 shorter events, 2.4 us)
Async XLA Ops:
  4.3 5.3 %copy-start.7 = (s32[64]{0:T(128)}, s32[64]{0:T(128)S(1)}, u32[]{:S(2)}) copy-start(s32[64]{0:T(128)S(1)} %dynamic_slice.6.slots) | copy-start | bytes 772
  5.2 1.6 copy-start.2
  6.8 2.9 copy-start.5
  9.7 2.0 copy-start.1
  11.7 8.1 %copy-start.15 = (bf16[1152,128]{1,0:T(8,128)(2,1)S(1)}, bf16[1152,128]{1,0:T(8,128)(2,1)}, u32[]{:S(2)}) copy-start(bf16[1152,128]{1,0:T(8,128)(2,1)} %refs_10_.1) | copy-start | bytes 884740
  11.7 9.1 %copy-start.14 = (bf16[1152,128]{1,0:T(8,128)(2,1)S(1)}, bf16[1152,128]{1,0:T(8,128)(2,1)}, u32[]{:S(2)}) copy-start(bf16[1152,128]{1,0:T(8,128)(2,1)} %refs_2_.1) | copy-start | bytes 884740
  11.7 61.4 %all-to-all-start = ((bf16[16,1024,128]{2,1,0:T(8,128)(2,1)}), bf16[16,1024,128]{2,1,0:T(8,128)(2,1)}, u32[]{:S(2)}, u32[]{:S(2)}) async-start(bf16[16,1024,128]{2,1,0:T(8,128)(2,1)} %bitcast.45), calls=%async_computation | async-start | bytes 8388608 | tf_op jit(solution)/shard_map/all_to_all | solution.py:818
  19.8 2.0 copy-start.12
  19.8 2.2 copy-start.13
  23.3 2.8 copy-start.11
  34.6 4.8 %copy-start.16 = (s32[1024,1]{0,1:T(1,128)S(1)}, s32[1024,1]{0,1:T(1,128)}, u32[]{:S(2)}) copy-start(s32[1024,1]{0,1:T(1,128)} %param.18) | copy-start | bytes 12292
  34.6 4.9 %copy-start.17 = (s32[1024]{0:T(1024)S(1)}, s32[1024]{0:T(1024)}, u32[]{:S(2)}) copy-start(s32[1024]{0:T(1024)} %param.19) | copy-start | bytes 12292
  39.7 0.5 copy-start.9
  76.6 1.0 copy-start.3
  168.9 1.2 copy-start.4
  170.1 0.7 copy-start.10
  172.5 2.0 copy-start
  174.5 135.9 %all-to-all-start.1 = ((bf16[16,1024,128]{2,1,0:T(8,128)(2,1)}), bf16[16,1024,128]{2,1,0:T(8,128)(2,1)}, u32[]{:S(2)}, u32[]{:S(2)}) async-start(bf16[16,1024,128]{2,1,0:T(8,128)(2,1)} %bitcast.44), calls=%async_computation.1 | async-start | bytes 8388608 | tf_op jit(solution)/shard_map/all_to_all | solution.py:850
  310.4 0.8 copy-start.6
  311.2 0.6 copy-start.8
